TPU v7x, 32 devices: a whole 2x2x4 slice. The times are simulated.
32 devices in a mesh: ta: 4 (over y, x), row: 4 (over z), col: 2 (over core).
Axes of the slice: x: 2, y: 2, z: 4, core: 2. Of those that a mesh axis runs over, the one named last changes fastest.
Arguments:
- latent_in: float32 [64, 64, 48, 384], P('ta', 'row', 'col'), may hold values from -6 to 6
- norm_gains: float32 [2, 384], replicated, may hold values from 0.1 to 1.9
- conv_weights: bfloat16 [2, 3, 3, 3, 384, 384], replicated, may hold values from -0.0625 to 0.0625
- conv_bias: float32 [2, 384], replicated, may hold values from -3 to 3
Outputs:
- latent_out: float32 [64, 64, 48, 384], P('ta', 'row', 'col')
All inputs are finite; a program needn't handle non-finite values.
Results may differ from a plain program's by a relative error of at most 0.002.
Values may be sent and summed in bfloat16 or wider, within the bound.
No kernel may reach another device: no remote copies, remote signals or barrier semaphores. Data moves between devices by JAX's collectives and lax.ppermute only.
A program may use at most 192 MiB of HBM per device.

v0:
```python
import jax
import jax.numpy as jnp
from jax import lax
from jax.sharding import PartitionSpec as P

EPS = 1e-06


def passed_along(x, axis, by):
    size = lax.axis_size(axis)
    pairs = [(i, i + by) for i in range(size) if 0 <= i + by < size]
    return lax.ppermute(x, axis, pairs)


def padded_2(cells, sides, width):
    for axis, dim in sides:
        count = lax.axis_size(axis)
        ends = count - 1
        head = lax.slice_in_dim(cells, 0, width, axis=dim)
        tail = lax.slice_in_dim(cells, cells.shape[dim] - width, cells.shape[dim], axis=dim)
        cells = jnp.concatenate(
            [
                lax.ppermute(tail, axis, [(i, (i + 1) % count) for i in range(ends)]),
                cells,
                lax.ppermute(head, axis, [((i + 1) % count, i) for i in range(ends)]),
            ],
            axis=dim,
        )
    return cells


def activate(value, gain):
    mean_sq = jnp.mean(value * value, axis=-1, keepdims=True)
    return jax.nn.silu(value * lax.rsqrt(mean_sq + EPS) * gain).astype(jnp.bfloat16)


def convolve(padded, weight, bias):
    frames = padded.shape[0] - 2
    height = padded.shape[1] - 2
    width = padded.shape[2] - 2
    chans = padded.shape[3]
    plane = (height + 2) * (width + 2)
    extra = 2 * (width + 2) + 2
    flat = padded.reshape(-1, chans)
    flat = jnp.concatenate([flat, jnp.zeros((extra, chans), flat.dtype)], axis=0)
    length = frames * plane
    total = jnp.zeros((length, weight.shape[-1]), jnp.float32)
    for tap_t in range(3):
        for tap_r in range(3):
            for tap_c in range(3):
                offset = tap_t * plane + tap_r * (width + 2) + tap_c
                piece = flat[offset : offset + length]
                total = total + jnp.dot(
                    piece, weight[tap_t, tap_r, tap_c], preferred_element_type=jnp.float32
                )
    grid = (total + bias).reshape(frames, height + 2, width + 2, -1)
    return grid[:, :height, :width]


def fetch(value, back, margin, gain):
    count = value.shape[0]
    moved = activate(value, gain)
    earlier = passed_along(moved[count - back :], "ta", 1)
    joined = jnp.concatenate([earlier, moved], axis=0)
    return padded_2(joined, (("row", 1), ("col", 2)), margin)


def shards(latent_in, norm_gains, conv_weights, conv_bias):
    first = convolve(fetch(latent_in, 2, 1, norm_gains[0]), conv_weights[0], conv_bias[0])
    second = convolve(fetch(first, 2, 1, norm_gains[1]), conv_weights[1], conv_bias[1])
    return latent_in + second


def solution(mesh):
    placed = (P("ta", "row", "col", None), P(), P(), P())
    return jax.shard_map(
        shards, mesh=mesh, in_specs=placed, out_specs=P("ta", "row", "col", None), check_vma=False
    )
```

profile of v0, /device:TPU:0, one launch (start us, length us, event | category | flops | bytes accessed | tf_op | source)
XLA Modules:
  0.0 696.6 jit_solution(6246900109891671936)
XLA Ops:
  14.5 12.5 %collective-permute-done = bf16[2,16,24,384]{3,2,1,0:T(8,128)(2,1)S(1)} collective-permute-done((bf16[2,16,24,384]{3,2,1,0:T(8,128)(2,1)S(1)}, bf16[2,16,24,384]{3,2,1,0:T(8,128)(2,1)S(1)}, u32[]{:S(2)}, u32[]{:S(2)}) %collective-permute-start) | collective-permute-done | bytes 589856 | tf_op jit(solution)/shard_map/ppermute | solution.py:12
  51.9 10.6 %pad_maximum_fusion = bf16[18,18,26,384]{3,2,1,0:T(8,128)(2,1)} fusion(bf16[18,18,1,384]{3,2,1,0:T(2,128)(2,1)S(1)} %collective-permute-done.4, bf16[18,1,24,384]{3,2,1,0:T(8,128)(2,1)S(1)} %collective-permute-done.2, bf16[16,16,24,384]{3,2,1,0:T(8,128)(2,1)S(1)} %multiply_convert_fusion.1, bf16[2,16,24,384]{3,2,1,0:T(8,128)(2,1)S(1)} %collective-permute-done, ...), kind=kLoop, calls=%fused_computation.59 | loop fusion | flops 38817792 | bytes 12939264 | tf_op jit(solution)/shard_map/concatenate | solution.py:21
  62.5 11.1 %reshape.36 = bf16[8424,384]{1,0:T(8,128)(2,1)} reshape(bf16[18,18,26,384]{3,2,1,0:T(8,128)(2,1)} %pad_maximum_fusion) | data formatting | bytes 12939264 | tf_op jit(solution)/shard_map/reshape | solution.py:44
  73.6 13.9 %fusion.85 = (bf16[16,18,26,384]{3,2,1,0:T(8,128)(2,1)}, bf16[16,18,26,384]{3,2,1,0:T(8,128)(2,1)}, bf16[16,18,26,384]{3,2,1,0:T(8,128)(2,1)}) fusion(bf16[18,18,26,384]{3,2,1,0:T(8,128)(2,1)} %pad_maximum_fusion), kind=kLoop, calls=%fused_computation.218 | loop fusion | bytes 34504704 | tf_op jit(solution)/shard_map/slice | solution.py:52
  87.5 9.9 %slice.442 = bf16[7488,384]{1,0:T(8,128)(2,1)} reshape(bf16[16,18,26,384]{3,2,1,0:T(8,128)(2,1)} %get-tuple-element.14) | data formatting | bytes 11501568 | tf_op jit(solution)/shard_map/slice | solution.py:52
  97.4 9.9 %slice.423 = bf16[7488,384]{1,0:T(8,128)(2,1)} reshape(bf16[16,18,26,384]{3,2,1,0:T(8,128)(2,1)} %get-tuple-element.15) | data formatting | bytes 11501568 | tf_op jit(solution)/shard_map/slice | solution.py:52
  107.3 9.8 %slice.403 = bf16[7488,384]{1,0:T(8,128)(2,1)} reshape(bf16[16,18,26,384]{3,2,1,0:T(8,128)(2,1)} %get-tuple-element.16) | data formatting | bytes 11501568 | tf_op jit(solution)/shard_map/slice | solution.py:52
  123.3 11.1 %convolution_add_fusion.51 = f32[7488,384]{1,0:T(8,128)} fusion(f32[7488,384]{1,0:T(8,128)S(1)} %fusion.34, bf16[7488,384]{1,0:T(8,128)(2,1)} %slice.403, bf16[3,3,3,384,384]{4,3,2,1,0:T(8,128)(2,1)} %get-tuple-element.10), kind=kOutput, calls=%fused_computation.51 | convolution fusion | flops 2211176448 | bytes 29048832 | tf_op jit(solution)/shard_map/dot_general | solution.py:53
  178.4 9.2 %convolution_add_fusion.44 = f32[7488,384]{1,0:T(8,128)} fusion(f32[7488,384]{1,0:T(8,128)} %convolution_add_fusion.45, bf16[8424,384]{1,0:T(8,128)(2,1)S(1)} %bitcast.175, bf16[3,3,3,384,384]{4,3,2,1,0:T(8,128)(2,1)} %get-tuple-element.10), kind=kOutput, calls=%fused_computation.44 | convolution fusion | flops 2211176448 | bytes 29048832 | tf_op jit(solution)/shard_map/dot_general | solution.py:53
  187.6 10.0 %convolution_add_fusion.43 = f32[7488,384]{1,0:T(8,128)S(1)} fusion(f32[7488,384]{1,0:T(8,128)} %convolution_add_fusion.44, bf16[7488,384]{1,0:T(8,128)(2,1)} %slice.423, bf16[3,3,3,384,384]{4,3,2,1,0:T(8,128)(2,1)} %get-tuple-element.10), kind=kOutput, calls=%fused_computation.43 | convolution fusion | flops 2211176448 | bytes 29048832 | tf_op jit(solution)/shard_map/dot_general | solution.py:53
  258.1 14.0 %convolution_add_fusion.34 = f32[7488,384]{1,0:T(8,128)} fusion(f32[7488,384]{1,0:T(8,128)} %convolution_add_fusion.35, bf16[7488,384]{1,0:T(8,128)(2,1)} %slice.442, bf16[3,3,3,384,384]{4,3,2,1,0:T(8,128)(2,1)} %get-tuple-element.10), kind=kOutput, calls=%fused_computation.34 | convolution fusion | flops 2211176448 | bytes 29048832 | tf_op jit(solution)/shard_map/dot_general | solution.py:53
  330.5 13.1 %reshape.37 = f32[16,18,26,384]{3,2,1,0:T(8,128)} reshape(f32[7488,384]{1,0:T(8,128)} %fusion) | data formatting | bytes 23003136 | tf_op jit(solution)/shard_map/reshape | solution.py:56
  358.5 13.5 %collective-permute-done.5 = bf16[2,16,24,384]{3,2,1,0:T(8,128)(2,1)S(1)} collective-permute-done((bf16[2,16,24,384]{3,2,1,0:T(8,128)(2,1)S(1)}, bf16[2,16,24,384]{3,2,1,0:T(8,128)(2,1)S(1)}, u32[]{:S(2)}, u32[]{:S(2)}) %collective-permute-start.5) | collective-permute-done | bytes 589856 | tf_op jit(solution)/shard_map/ppermute | solution.py:12
  393.5 10.8 %pad_maximum_fusion.1 = bf16[18,18,26,384]{3,2,1,0:T(8,128)(2,1)} fusion(bf16[18,18,1,384]{3,2,1,0:T(2,128)(2,1)S(1)} %collective-permute-done.9, bf16[18,1,24,384]{3,2,1,0:T(8,128)(2,1)S(1)} %collective-permute-done.7, bf16[16,16,24,384]{3,2,1,0:T(8,128)(2,1)S(1)} %multiply_convert_fusion, bf16[2,16,24,384]{3,2,1,0:T(8,128)(2,1)S(1)} %collective-permute-done.5, ...), kind=kLoop, calls=%fused_computation.60 | loop fusion | flops 38817792 | bytes 12939264 | tf_op jit(solution)/shard_map/concatenate | solution.py:21
  404.3 11.1 %reshape.38 = bf16[8424,384]{1,0:T(8,128)(2,1)} reshape(bf16[18,18,26,384]{3,2,1,0:T(8,128)(2,1)} %pad_maximum_fusion.1) | data formatting | bytes 12939264 | tf_op jit(solution)/shard_map/reshape | solution.py:44
  415.4 13.9 %fusion.84 = (bf16[16,18,26,384]{3,2,1,0:T(8,128)(2,1)}, bf16[16,18,26,384]{3,2,1,0:T(8,128)(2,1)}, bf16[16,18,26,384]{3,2,1,0:T(8,128)(2,1)}) fusion(bf16[18,18,26,384]{3,2,1,0:T(8,128)(2,1)} %pad_maximum_fusion.1), kind=kLoop, calls=%fused_computation.217 | loop fusion | bytes 34504704 | tf_op jit(solution)/shard_map/slice | solution.py:52
  429.3 9.9 %slice.508 = bf16[7488,384]{1,0:T(8,128)(2,1)} reshape(bf16[16,18,26,384]{3,2,1,0:T(8,128)(2,1)} %get-tuple-element.11) | data formatting | bytes 11501568 | tf_op jit(solution)/shard_map/slice | solution.py:52
  439.1 9.9 %slice.489 = bf16[7488,384]{1,0:T(8,128)(2,1)} reshape(bf16[16,18,26,384]{3,2,1,0:T(8,128)(2,1)} %get-tuple-element.12) | data formatting | bytes 11501568 | tf_op jit(solution)/shard_map/slice | solution.py:52
  449.0 9.8 %slice.469 = bf16[7488,384]{1,0:T(8,128)(2,1)} reshape(bf16[16,18,26,384]{3,2,1,0:T(8,128)(2,1)} %get-tuple-element.13) | data formatting | bytes 11501568 | tf_op jit(solution)/shard_map/slice | solution.py:52
  464.9 11.1 %convolution_add_fusion.25 = f32[7488,384]{1,0:T(8,128)} fusion(f32[7488,384]{1,0:T(8,128)S(1)} %fusion.17, bf16[7488,384]{1,0:T(8,128)(2,1)} %slice.469, bf16[3,3,3,384,384]{4,3,2,1,0:T(8,128)(2,1)} %get-tuple-element.9), kind=kOutput, calls=%fused_computation.25 | convolution fusion | flops 2211176448 | bytes 29048832 | tf_op jit(solution)/shard_map/dot_general | solution.py:53
  529.1 10.0 %convolution_add_fusion.17 = f32[7488,384]{1,0:T(8,128)S(1)} fusion(f32[7488,384]{1,0:T(8,128)} %convolution_add_fusion.18, bf16[7488,384]{1,0:T(8,128)(2,1)} %slice.489, bf16[3,3,3,384,384]{4,3,2,1,0:T(8,128)(2,1)} %get-tuple-element.9), kind=kOutput, calls=%fused_computation.17 | convolution fusion | flops 2211176448 | bytes 29048832 | tf_op jit(solution)/shard_map/dot_general | solution.py:53
  599.5 14.0 %convolution_add_fusion.8 = f32[7488,384]{1,0:T(8,128)} fusion(f32[7488,384]{1,0:T(8,128)} %convolution_add_fusion.9, bf16[7488,384]{1,0:T(8,128)(2,1)} %slice.508, bf16[3,3,3,384,384]{4,3,2,1,0:T(8,128)(2,1)} %get-tuple-element.9), kind=kOutput, calls=%fused_computation.8 | convolution fusion | flops 2211176448 | bytes 29048832 | tf_op jit(solution)/shard_map/dot_general | solution.py:53
  671.9 13.1 %reshape.39 = f32[16,18,26,384]{3,2,1,0:T(8,128)} reshape(f32[7488,384]{1,0:T(8,128)} %fusion.1) | data formatting | bytes 23003136 | tf_op jit(solution)/shard_map/reshape | solution.py:56
  685.1 11.3 %slice_add_fusion = f32[16,16,24,384]{3,2,1,0:T(8,128)} fusion(f32[16,16,24,384]{3,2,1,0:T(8,128)} %param.4, f32[16,18,26,384]{3,2,1,0:T(8,128)} %reshape.39), kind=kLoop, calls=%fused_computation.54 | loop fusion | flops 2359296 | bytes 28311552 | tf_op jit(solution)/shard_map/add | solution.py:71
  (109 shorter events, 422.1 us)
Async XLA Ops:
  0.0 6.4 copy-start
  6.4 38.7 %slice-start.4 = ((s8[15925248]{0:T(1024)(128)(4,1)}), s8[3342336]{0:T(1024)(128)(4,1)S(1)}, s32[]{:S(2)}) async-start(s8[15925248]{0:T(1024)(128)(4,1)} %bitcast.176), calls=%async_computation.4 | async-start | bytes 6684672
  6.5 38.6 %slice-start.5 = ((s8[15925248]{0:T(1024)(128)(4,1)}), s8[4194304]{0:T(1024)(128)(4,1)S(1)}, s32[]{:S(2)}) async-start(s8[15925248]{0:T(1024)(128)(4,1)} %bitcast.176), calls=%async_computation.5 | async-start | bytes 8388608
  6.5 38.6 %slice-start.6 = ((s8[15925248]{0:T(1024)(128)(4,1)}), s8[4194304]{0:T(1024)(128)(4,1)S(1)}, s32[]{:S(2)}) async-start(s8[15925248]{0:T(1024)(128)(4,1)} %bitcast.176), calls=%async_computation.6 | async-start | bytes 8388608
  9.3 35.8 %slice-start.7 = ((s8[15925248]{0:T(1024)(128)(4,1)}), s8[4194304]{0:T(1024)(128)(4,1)S(1)}, s32[]{:S(2)}) async-start(s8[15925248]{0:T(1024)(128)(4,1)} %bitcast.176), calls=%async_computation.7 | async-start | bytes 8388608
  9.3 17.7 %collective-permute-start = (bf16[2,16,24,384]{3,2,1,0:T(8,128)(2,1)S(1)}, bf16[2,16,24,384]{3,2,1,0:T(8,128)(2,1)S(1)}, u32[]{:S(2)}, u32[]{:S(2)}) collective-permute-start(bf16[2,16,24,384]{3,2,1,0:T(8,128)(2,1)S(1)} %slice.528), channel_id=1, source_target_pairs={{0,8},{8,16},{16,24},{1,9},{9,17},{17,25},{2,10},{10,18},{18,26},{... | collective-permute-start | bytes 1769480 | tf_op jit(solution)/shard_map/ppermute | solution.py:12
  27.1 9.7 %collective-permute-start.1 = (bf16[18,1,24,384]{3,2,1,0:T(8,128)(2,1)S(1)}, bf16[18,1,24,384]{3,2,1,0:T(8,128)(2,1)S(1)}, u32[]{:S(2)}, u32[]{:S(2)}) collective-permute-start(bf16[18,1,24,384]{3,2,1,0:T(8,128)(2,1)S(1)} %get-tuple-element.23), channel_id=1, source_target_pairs={{0,2},{2,4},{4,6},{1,3},{3,5},{5,7},{8,10},{10,12},{12,14},{9,11},... | collective-permute-start | bytes 995336 | tf_op jit(solution)/shard_map/ppermute | solution.py:23
  30.6 10.3 %collective-permute-start.2 = (bf16[18,1,24,384]{3,2,1,0:T(8,128)(2,1)S(1)}, bf16[18,1,24,384]{3,2,1,0:T(8,128)(2,1)S(1)}, u32[]{:S(2)}, u32[]{:S(2)}) collective-permute-start(bf16[18,1,24,384]{3,2,1,0:T(8,128)(2,1)S(1)} %get-tuple-element.24), channel_id=1, source_target_pairs={{2,0},{4,2},{6,4},{3,1},{5,3},{7,5},{10,8},{12,10},{14,12},{11,9},... | collective-permute-start | bytes 995336 | tf_op jit(solution)/shard_map/ppermute | solution.py:25
  42.1 9.8 %collective-permute-start.3 = (bf16[18,18,1,384]{3,2,1,0:T(2,128)(2,1)S(1)}, bf16[18,18,1,384]{3,2,1,0:T(2,128)(2,1)S(1)}, u32[]{:S(2)}, u32[]{:S(2)}) collective-permute-start(bf16[18,18,1,384]{3,2,1,0:T(2,128)(2,1)S(1)} %get-tuple-element.19), channel_id=1, source_target_pairs={{0,1},{2,3},{4,5},{6,7},{8,9},{10,11},{12,13},{14,15},{16,17},{18,... | collective-permute-start | bytes 746504 | tf_op jit(solution)/shard_map/ppermute | solution.py:23
  43.4 7.9 %copy-start.4 = (f32[2,384]{1,0:T(2,128)S(1)}, f32[2,384]{1,0:T(2,128)}, u32[]{:S(2)}) copy-start(f32[2,384]{1,0:T(2,128)} %param.7) | copy-start | bytes 9220
  43.5 8.5 %collective-permute-start.4 = (bf16[18,18,1,384]{3,2,1,0:T(2,128)(2,1)S(1)}, bf16[18,18,1,384]{3,2,1,0:T(2,128)(2,1)S(1)}, u32[]{:S(2)}, u32[]{:S(2)}) collective-permute-start(bf16[18,18,1,384]{3,2,1,0:T(2,128)(2,1)S(1)} %get-tuple-element.20), channel_id=1, source_target_pairs={{1,0},{3,2},{5,4},{7,6},{9,8},{11,10},{13,12},{15,14},{17,16},{19,... | collective-permute-start | bytes 746504 | tf_op jit(solution)/shard_map/ppermute | solution.py:25
  117.1 17.3 %slice-start.2 = ((s8[6469632]{0:T(1024)(128)(4,1)}), s8[4194304]{0:T(1024)(128)(4,1)S(1)}, s32[]{:S(2)}) async-start(s8[6469632]{0:T(1024)(128)(4,1)} %bitcast.174), calls=%async_computation.2 | async-start | bytes 8388608
  123.3 11.1 %slice-start.3 = ((s8[6469632]{0:T(1024)(128)(4,1)}), s8[2275328]{0:T(1024)(128)(4,1)S(1)}, s32[]{:S(2)}) async-start(s8[6469632]{0:T(1024)(128)(4,1)} %bitcast.174), calls=%async_computation.3 | async-start | bytes 4550656
  315.8 7.0 copy-start.2
  343.6 4.7 copy-start.3
  354.1 17.9 %collective-permute-start.5 = (bf16[2,16,24,384]{3,2,1,0:T(8,128)(2,1)S(1)}, bf16[2,16,24,384]{3,2,1,0:T(8,128)(2,1)S(1)}, u32[]{:S(2)}, u32[]{:S(2)}) collective-permute-start(bf16[2,16,24,384]{3,2,1,0:T(8,128)(2,1)S(1)} %slice.576), channel_id=1, source_target_pairs={{0,8},{8,16},{16,24},{1,9},{9,17},{17,25},{2,10},{10,18},{18,26},{... | collective-permute-start | bytes 1769480 | tf_op jit(solution)/shard_map/ppermute | solution.py:12
  372.1 11.0 %collective-permute-start.6 = (bf16[18,1,24,384]{3,2,1,0:T(8,128)(2,1)S(1)}, bf16[18,1,24,384]{3,2,1,0:T(8,128)(2,1)S(1)}, u32[]{:S(2)}, u32[]{:S(2)}) collective-permute-start(bf16[18,1,24,384]{3,2,1,0:T(8,128)(2,1)S(1)} %get-tuple-element.21), channel_id=1, source_target_pairs={{0,2},{2,4},{4,6},{1,3},{3,5},{5,7},{8,10},{10,12},{12,14},{9,11},... | collective-permute-start | bytes 995336 | tf_op jit(solution)/shard_map/ppermute | solution.py:23
  375.5 11.6 %collective-permute-start.7 = (bf16[18,1,24,384]{3,2,1,0:T(8,128)(2,1)S(1)}, bf16[18,1,24,384]{3,2,1,0:T(8,128)(2,1)S(1)}, u32[]{:S(2)}, u32[]{:S(2)}) collective-permute-start(bf16[18,1,24,384]{3,2,1,0:T(8,128)(2,1)S(1)} %get-tuple-element.22), channel_id=1, source_target_pairs={{2,0},{4,2},{6,4},{3,1},{5,3},{7,5},{10,8},{12,10},{14,12},{11,9},... | collective-permute-start | bytes 995336 | tf_op jit(solution)/shard_map/ppermute | solution.py:25
  388.4 2.8 collective-permute-start.8
  389.7 3.8 collective-permute-start.9
  458.9 17.2 %slice-start = ((s8[6469632]{0:T(1024)(128)(4,1)}), s8[4194304]{0:T(1024)(128)(4,1)S(1)}, s32[]{:S(2)}) async-start(s8[6469632]{0:T(1024)(128)(4,1)} %bitcast.172), calls=%async_computation | async-start | bytes 8388608
  464.9 11.1 %slice-start.1 = ((s8[6469632]{0:T(1024)(128)(4,1)}), s8[2275328]{0:T(1024)(128)(4,1)S(1)}, s32[]{:S(2)}) async-start(s8[6469632]{0:T(1024)(128)(4,1)} %bitcast.172), calls=%async_computation.1 | async-start | bytes 4550656
  657.3 7.0 copy-start.1
where the time goes:
time: 705 us; the launch traced here: 697 us
  matrix products  426 us (60%)
  local copies, waits for them, and re-layouts  144 us (20%)
  other arithmetic  53.3 us (8%)
  waiting for transfers between devices  47.8 us (7%)
  starting transfers between devices  24.6 us (3%)
    dot_general x54, matrix products, convolve(): jnp.dot(piece, weight[tap_t, tap_r, tap_c], preferred_element_type=jnp.fl...  426 us
    slice x8, local copies, waits for them, and re-layouts, convolve(): piece = flat[offset:offset + length]  86.9 us
    reshape x2, local copies, waits for them, and re-layouts, convolve(): grid = (total + bias).reshape(frames, height + 2, width + 2, -1)  26.3 us
    ppermute x2, waiting for transfers between devices, passed_along(): return lax.ppermute(x, axis, pairs)  26 us
    reshape x2, local copies, waits for them, and re-layouts, convolve(): flat = padded.reshape(-1, chans)  22.2 us
    concatenate x2, other arithmetic, padded_2(): jnp.concatenate([lax.ppermute(tail, axis, [(i, (i + 1) % count) for i in...  21.4 us
  transfers between devices with their start and end apart: 10, of which 8 were waited for; matrix products, arithmetic and copies ran while one was open for 1% of the time, Pallas kernels for 0%

commit v1 on v0

v1 whole, which is shorter than its diff:
```python
import jax
import jax.numpy as jnp
from jax import lax
from jax.experimental import pallas as pl
from jax.experimental.pallas import tpu as pltpu
from jax.sharding import PartitionSpec as P

EPS = 1e-06
PARITY = True
SUB = 8
LANE = 128
F32 = jnp.float32
BF16 = jnp.bfloat16


def activate(value, gain):
    mean_sq = jnp.mean(value * value, axis=-1, keepdims=True)
    u = value * lax.rsqrt(mean_sq + EPS) * gain
    return (u / (1.0 + jnp.exp(-u))).astype(BF16)


def border_parts(value, r, j, half, blocks, last_valid):
    parts = []
    if r == 0:
        parts.append(("row", 0, j * SUB, value[0:SUB]))
    if r == half - 1:
        parts.append(("row", 1, j * SUB, value[SUB:16]))
    if j == 0:
        parts.append(("col", 0, r, value[0:1]))
        parts.append(("col", 0, r + half, value[SUB : SUB + 1]))
    if j == blocks - 1:
        parts.append(("col", 1, r, value[last_valid : last_valid + 1]))
        parts.append(("col", 1, r + half, value[SUB + last_valid : SUB + last_valid + 1]))
    return parts


def prepare_kernel(last_valid, x_ref, gain_ref, out_ref, row0, row1, col0, col1, tail_ref, row_f, col_f):
    half, blocks = x_ref.shape[1] // 2, x_ref.shape[2] // SUB
    gain = gain_ref[...]
    for r in range(half):
        for j in range(blocks):
            cols = pl.ds(j * SUB, SUB)
            v = jnp.concatenate([x_ref[0, r, cols, :], x_ref[0, r + half, cols, :]], axis=0)
            a = activate(v, gain)
            out_ref[0, pl.ds((r * blocks + j) * 16, 16), :] = a
            tail_ref[0, pl.ds((r * blocks + j) * 16, 16), :] = a
            for kind, e, row, piece in border_parts(a.astype(F32), r, j, half, blocks, last_valid):
                dst = row_f if kind == "row" else col_f
                dst[e, pl.ds(row, piece.shape[0]), :] = piece
    row0[0] = row_f[0].astype(BF16)
    row1[0] = row_f[1].astype(BF16)
    col0[0] = col_f[0].astype(BF16)
    col1[0] = col_f[1].astype(BF16)


def prepare(x, gain, width):
    frames, rows, cols, chans = x.shape
    cells = rows * cols

    def spec(n):
        return pl.BlockSpec((1, n, chans), lambda f: (f, 0, 0))

    sizes = (cells, cols, cols, rows, rows)
    return pl.pallas_call(
        lambda *refs: prepare_kernel((width - 1) % SUB, *refs),
        out_shape=[jax.ShapeDtypeStruct((frames, n, chans), BF16) for n in sizes]
        + [jax.ShapeDtypeStruct((2, cells, chans), BF16)],
        grid=(frames,),
        in_specs=[
            pl.BlockSpec((1, rows, cols, chans), lambda f: (f, 0, 0, 0)),
            pl.BlockSpec((1, chans), lambda f: (0, 0)),
        ],
        out_specs=[spec(n) for n in sizes]
        + [pl.BlockSpec((1, cells, chans), lambda f: (jnp.maximum(f - (frames - 2), 0), 0, 0))],
        scratch_shapes=[pltpu.VMEM((2, cols, chans), F32), pltpu.VMEM((2, rows, chans), F32)],
        compiler_params=pltpu.CompilerParams(vmem_limit_bytes=60 << 20),
        cost_estimate=pl.CostEstimate(flops=20 * x.size, bytes_accessed=6 * x.size, transcendentals=2 * x.size),
        name="prepare",
    )(x, gain)


def conv_kernel(cfg, *refs):
    segs, n_ops, n_in, rows, blocks, chans, layer, last_valid, final, x_start = cfg
    n_out = n_in - 2
    steps = n_out // 2
    half = rows // 2
    cols = blocks * SUB
    wide = blocks * 16
    n_chunk = chans // LANE
    ins = refs[:n_ops]
    at = n_ops
    flag_ref, parity_ref, w_hbm, bias_ref, gain_ref = refs[at : at + 5]
    at += 5
    if final:
        x_hbm = refs[at]
        at += 2 if final == 2 else 1
        outs = refs[at : at + 1]
        at += 1
    else:
        outs = refs[at : at + 6]
        at += 6
    (a_buf, w_buf, t_buf, edge_buf, side_buf, corner_buf, edge_f, side_f, corner_f, pm, p3, o_buf,
     row_f, col_f, row_buf, col_buf, in_sem, w_sem, x_sem, o_sem, b_sem) = refs[at:]
    taps = [(dt, dr, dc) for dt in range(3) for dr in range(3) for dc in range(3)]
    slots = (parity_ref[0], 1 - parity_ref[0])

    copies = []

    def fetch(src, dst):
        copies.append(pltpu.make_async_copy(src, dst, in_sem.at[len(copies)]))

    base = 0
    corner_at = 0
    corners = []
    for kind, which, start, count in segs:
        here = pl.ds(base, count)
        if kind == "own":
            t, top, bot, lft, rgt = [ins[n] for n in which]
            there = pl.ds(start, count)
            fetch(t.at[there], t_buf.at[here])
            frames = t.shape[0]
            extra = top.shape[0] - frames
            for e, part in ((0, top), (1, bot)):
                fetch(part.at[there], edge_buf.at[e, here])
                fetch(part.at[pl.ds(frames, extra)], corner_buf.at[e, pl.ds(corner_at, extra)])
                corners.append((e, e, corner_at, extra, 2 * start, base, count))
            for e, part in ((0, lft), (1, rgt)):
                fetch(part.at[there], side_buf.at[e, here])
            corner_at += extra
        else:
            t, rec = [ins[n] for n in which]
            fetch(t, t_buf.at[here])
            for e in range(2):
                fetch(rec.at[:, pl.ds(e * cols, cols)], edge_buf.at[e, here])
                fetch(rec.at[:, pl.ds(2 * cols + e * rows, rows)], side_buf.at[e, here])
            fetch(rec.at[:, pl.ds(2 * (cols + rows), SUB)], corner_buf.at[0, pl.ds(corner_at, count), pl.ds(0, SUB)])
            for e in range(2):
                for k in range(count):
                    corners.append((e, 0, corner_at + k, 1, 2 * e, base + k, 1))
            corner_at += count
        base += count
    w_copies = [
        pltpu.make_async_copy(
            w_hbm.at[layer, dt, :, :, :, pl.ds(oc * LANE, LANE)], w_buf.at[oc, dt], w_sem.at[dt, oc]
        )
        for dt in range(3)
        for oc in range(n_chunk)
    ]
    for c in copies:
        c.start()
    for c in w_copies:
        c.start()
    if final:
        x_copy = pltpu.make_async_copy(x_hbm.at[pl.ds(x_start, n_out)], o_buf, x_sem)
        x_copy.start()
    for c in copies:
        c.wait()

    def widen(f, carry):
        for e in range(2):
            edge_f[e, f] = edge_buf[e, f].astype(F32)
            side_f[e, f] = side_buf[e, f].astype(F32) * flag_ref[e]
        return carry

    lax.fori_loop(0, n_in, widen, 0)
    for e, source, where, extra, first, base_, count in corners:
        block = corner_buf[source, pl.ds(where, extra)].astype(F32).reshape(extra * cols, chans)
        corner_f[e, pl.ds(2 * base_, 2 * count), :] = block[first : first + 2 * count]

    sub_index = lax.broadcasted_iota(jnp.int32, (SUB, chans), 0)
    is_first = sub_index == 0
    is_last = sub_index == SUB - 1
    is_valid_last = sub_index == last_valid

    def tile_at(f, r, j):
        return t_buf[f, pl.ds((r * blocks + j) * 16, 16), :]

    def beside(e, f, row):
        if row < 0 or row >= rows:
            value = corner_f[slots[0 if row < 0 else 1], pl.ds(2 * f + e, 1), :] * flag_ref[e]
        else:
            value = side_f[e, f, pl.ds(row, 1), :]
        return jnp.broadcast_to(value, (SUB, chans))

    def build(f, rs):
        tiles = []
        for j in range(blocks):
            if 1 <= rs <= half:
                tiles.append(tile_at(f, rs - 1, j))
            elif rs == 0:
                upper = edge_f[slots[0], f, pl.ds(j * SUB, SUB), :]
                lower = tile_at(f, half - 1, j).astype(F32)[0:SUB]
                tiles.append(jnp.concatenate([upper, lower], axis=0).astype(BF16))
            else:
                upper = tile_at(f, 0, j).astype(F32)[SUB:16]
                lower = edge_f[slots[1], f, pl.ds(j * SUB, SUB), :]
                tiles.append(jnp.concatenate([upper, lower], axis=0).astype(BF16))
        shifted = [[[None, None] for _ in range(blocks)] for _ in range(2)]
        for h in range(2):
            row = rs - 1 + half * h
            left = beside(0, f, row)
            right = beside(1, f, row)
            parts = [t.astype(F32)[h * SUB : (h + 1) * SUB] for t in tiles]
            down = [left] + [pltpu.roll(p, 1, 0) for p in parts]
            up = [pltpu.roll(p, SUB - 1, 0) for p in parts]
            for j in range(blocks):
                shifted[0][j][h] = jnp.where(is_first, down[j], down[j + 1])
                if j + 1 < blocks:
                    shifted[1][j][h] = jnp.where(is_last, up[j + 1], up[j])
                else:
                    shifted[1][j][h] = jnp.where(is_valid_last, right, up[j])
        stores = []
        for j in range(blocks):
            low = jnp.concatenate(shifted[0][j], axis=0).astype(BF16)
            high = jnp.concatenate(shifted[1][j], axis=0).astype(BF16)
            for dc, value in ((0, low), (1, tiles[j]), (2, high)):
                for kc in range(n_chunk):
                    part = value[:, kc * LANE : (kc + 1) * LANE]
                    stores.append((a_buf, (kc, dc, f, rs, pl.ds(j * 16, 16), slice(None)), part))
        return stores

    def put(stores):
        for ref, index, value in stores:
            ref[index] = value

    def finish(q, f, r, j, live=None):
        if r == half:
            stores = []
            for e in range(2):
                stores.append((row_buf, (e, f), row_f[q, e].astype(BF16)))
                stores.append((col_buf, (e, f), col_f[q, e].astype(BF16)))
            return stores
        sl = pl.ds(j * 16, 16)
        v = jnp.concatenate([pm[q, r, sl, :], p3[q, r, sl, :]], axis=1) + bias_ref[...]
        if not final:
            a = activate(v, gain_ref[...])
            stores = [(o_buf, (f, pl.ds((r * blocks + j) * 16, 16), slice(None)), a)]
            for kind, e, row, piece in border_parts(a.astype(F32), r, j, half, blocks, last_valid):
                dst = row_f if kind == "row" else col_f
                stores.append((dst, (q, e, pl.ds(row, piece.shape[0]), slice(None)), piece))
            return stores
        stores = []
        for h in range(2):
            index = (f, r + half * h, pl.ds(j * SUB, SUB), slice(None))
            part = v[h * SUB : (h + 1) * SUB]
            if live is not None:
                part = jnp.where(live, part, 0.0)
            stores.append((o_buf, index, o_buf[index] + part))
        return stores

    units = [(r, j) for r in range(half) for j in range(blocks)]
    if not final:
        units.append((half, 0))

    main_chunks = [(tap, kc) for tap in taps for kc in range(n_chunk)]
    pair_chunks = [
        ((dt, drp, dc), kc)
        for dt in range(3) for drp in range(4) for dc in range(3) for kc in range(n_chunk)
    ]

    def main_weight(chunk):
        if chunk is None:
            return jnp.zeros((LANE, 2 * LANE), BF16)
        (dt, dr, dc), kc = chunk
        here = pl.ds(kc * LANE, LANE)
        return jnp.concatenate([w_buf[0, dt, dr, dc, here, :], w_buf[1, dt, dr, dc, here, :]], axis=1)

    def pair_weight(chunk):
        (dt, drp, dc), kc = chunk
        sides = []
        for dr in (drp, drp - 1):
            if 0 <= dr <= 2:
                sides.append(w_buf[2, dt, dr, dc, pl.ds(kc * LANE, LANE), :])
            else:
                sides.append(jnp.zeros((LANE, LANE), BF16))
        return jnp.concatenate(sides, axis=1)

    def lhs_piece(chunk, o, r):
        (dt, dr, dc), kc = chunk
        return a_buf[kc, dc, o + dt, r + dr]

    def run_pass(chunks, k, weight, accs, o, row_of):
        one = chunks[2 * k]
        two = chunks[2 * k + 1] if 2 * k + 1 < len(chunks) else None
        w = jnp.concatenate([weight(one), weight(two)], axis=0)
        reg = k % 2
        for q in range(2):
            pltpu.matmul_push_rhs(w, staging_register=reg, mxu_index=q)
        for n in range(len(accs[0])):
            for q in range(2):
                a = lhs_piece(one, o + q, row_of(n))
                b = lhs_piece(two, o + q, row_of(n)) if two is not None else a
                pltpu.matmul_acc_lhs(
                    accs[q][n], jnp.concatenate([a, b], axis=1), load_staged_rhs=reg if n == 0 else None
                )

    n_main = (len(main_chunks) + 1) // 2
    n_pair = len(pair_chunks) // 2

    def pop_main(accs, q, r):
        pm[q, r] = pltpu.matmul_pop(accs[q][r])

    def pop_pair(accs, q, n):
        v = pltpu.matmul_pop(accs[q][n])
        p3[q, 2 * n] = v[:, :LANE]
        p3[q, 2 * n + 1] = v[:, LANE:]

    def share(todo, k, lead, span):
        k -= lead
        if k < 0 or k >= span:
            return []
        return todo[k * len(todo) // span : (k + 1) * len(todo) // span]

    def out_copy(i):
        here = pl.ds(2 * i, 2)
        there = here if not final else pl.ds(x_start + 2 * i, 2)
        return pltpu.make_async_copy(o_buf.at[here], outs[0].at[there], o_sem.at[i])

    def body(main_accs, pair_accs):
        for q in range(2):
            for acc in main_accs[q] + pair_accs[q]:
                pltpu.matmul_pop(acc)

        def first_frames(f, carry):
            for rs in range(half + 2):
                put(build(f, rs))
            return carry

        lax.fori_loop(0, min(4, n_in), first_frames, 0)
        for c in w_copies:
            c.wait()
        if final:
            x_copy.wait()

        def step(i, carry):
            o = 2 * i
            done = jnp.maximum(o - 2, 0)
            live = i > 0
            todo = [(q, r, j) for q in range(2) for r, j in units]
            lead = 3
            pending = []
            for k in range(n_main):
                run_pass(main_chunks, k, main_weight, main_accs, o, lambda n: n)
                if k == 1:
                    for q in range(2):
                        for n in range(half // 2):
                            pop_pair(pair_accs, q, n)
                put(pending)
                pending = []
                for q, r, j in share(todo, k, lead, n_main - lead - 2):
                    if r == half:
                        put(pending)
                        pending = []
                    pending += finish(q, done + q, r, j, live)
            put(pending)

            new = jnp.minimum(o + 4, n_in - 2)
            todo = [(q, rs) for q in range(2) for rs in range(half + 2)]
            lead = 10
            pending = []
            for k in range(n_pair):
                run_pass(pair_chunks, k, pair_weight, pair_accs, o, lambda n: 2 * n)
                if 4 <= k < 4 + half // 2:
                    for q in range(2):
                        for r in range(2 * (k - 4), 2 * (k - 4) + 2):
                            pop_main(main_accs, q, r)
                put(pending)
                pending = []
                for q, rs in share(todo, k, lead, n_pair - lead - 2):
                    pending += build(new + q, rs)
            put(pending)

            @pl.when(i > 0)
            def _():
                out_copy(i - 1).start()

            return carry

        lax.fori_loop(0, steps, step, 0)
        for q in range(2):
            for n in range(half // 2):
                pop_pair(pair_accs, q, n)
        for q in range(2):
            for r, j in units:
                put(finish(q, n_out - 2 + q, r, j))
        last = [out_copy(steps - 1)]
        if not final:
            for e in range(2):
                last.append(pltpu.make_async_copy(row_buf.at[e], outs[1 + e], b_sem.at[e]))
                last.append(pltpu.make_async_copy(col_buf.at[e], outs[3 + e], b_sem.at[2 + e]))
            last.append(pltpu.make_async_copy(o_buf.at[pl.ds(n_out - 2, 2)], outs[5], b_sem.at[4]))
        for c in last:
            c.start()
        for i in range(steps - 1):
            out_copy(i).wait()
        for c in last:
            c.wait()

    pl.run_scoped(
        body,
        tuple(tuple(pltpu.ACC(q)((wide, 2 * LANE), F32) for _ in range(half)) for q in range(2)),
        tuple(tuple(pltpu.ACC(q)((wide, 2 * LANE), F32) for _ in range(half // 2)) for q in range(2)),
    )


def conv(segments, flags, parity, weights, bias, gain, layer, rows, width, x=None, x_start=0, into=None):
    blocks = -(-width // SUB)
    cols = blocks * SUB
    chans = weights.shape[-1]
    operands, cfg_segs = [], []
    corner_rows = 0
    for kind, arrays, start, count in segments:
        which = []
        for a in arrays:
            known = [n for n, b in enumerate(operands) if b is a]
            if not known:
                operands.append(a)
            which.append(known[0] if known else len(operands) - 1)
        cfg_segs.append((kind, tuple(which), start, count))
        corner_rows += arrays[1].shape[0] - arrays[0].shape[0] if kind == "own" else count
    n_ops = len(operands)
    n_in = sum(count for _, _, _, count in segments)
    n_out = n_in - 2
    half = rows // 2
    wide = blocks * 16
    final = 0 if x is None else (1 if into is None else 2)
    cfg = (tuple(cfg_segs), n_ops, n_in, rows, blocks, chans, layer, (width - 1) % SUB, final, x_start)
    any_spec = pl.BlockSpec(memory_space=pltpu.HBM)
    vmem_spec = pl.BlockSpec(memory_space=pltpu.VMEM)
    operands += [flags, parity, weights, bias, gain]
    in_specs = [any_spec] * n_ops + [pl.BlockSpec(memory_space=pltpu.SMEM)] * 2 + [any_spec, vmem_spec, vmem_spec]
    aliases = {}
    if final:
        operands.append(x)
        in_specs.append(any_spec)
        if final == 2:
            aliases = {len(operands): 0}
            operands.append(into)
            in_specs.append(any_spec)
        out_shape = [jax.ShapeDtypeStruct(x.shape, F32)]
        o_buf = pltpu.VMEM((n_out, rows, cols, chans), F32)
    else:
        out_shape = [
            jax.ShapeDtypeStruct((n_out, n, chans), BF16) for n in (rows * cols, cols, cols, rows, rows)
        ]
        out_shape.append(jax.ShapeDtypeStruct((2, rows * cols, chans), BF16))
        o_buf = pltpu.VMEM((n_out, rows * cols, chans), BF16)
    n_border = 1 if final else n_out
    copies = sum(7 if kind == "own" else 6 for kind, _, _, count in segments)
    scratch = [
        ((chans // LANE, 3, n_in, half + 2, wide, LANE), BF16),
        ((chans // LANE, 3, 3, 3, chans, LANE), BF16),
        ((n_in, rows * cols, chans), BF16),
        ((2, n_in, cols, chans), BF16),
        ((2, n_in, rows, chans), BF16),
        ((2, corner_rows, cols, chans), BF16),
        ((2, n_in, cols, chans), F32),
        ((2, n_in, rows, chans), F32),
        ((2, 2 * n_in, chans), F32),
        ((2, half, wide, 2 * LANE), F32),
        ((2, half, wide, LANE), F32),
        (o_buf.shape, o_buf.dtype),
        ((2, 2, cols, chans), F32),
        ((2, 2, rows, chans), F32),
        ((2, n_border, cols, chans), BF16),
        ((2, n_border, rows, chans), BF16),
    ]
    cells = n_out * rows * cols
    out = pl.pallas_call(
        lambda *refs: conv_kernel(cfg, *refs),
        out_shape=out_shape,
        in_specs=in_specs,
        out_specs=[any_spec] * len(out_shape),
        scratch_shapes=[pltpu.VMEM(shape, dtype) for shape, dtype in scratch]
        + [
            pltpu.SemaphoreType.DMA((copies,)),
            pltpu.SemaphoreType.DMA((3, chans // LANE)),
            pltpu.SemaphoreType.DMA,
            pltpu.SemaphoreType.DMA((n_out // 2,)),
            pltpu.SemaphoreType.DMA((5,)),
        ],
        input_output_aliases=aliases,
        compiler_params=pltpu.CompilerParams(vmem_limit_bytes=60 << 20),
        cost_estimate=pl.CostEstimate(
            flops=2 * 27 * cells * chans * chans, bytes_accessed=8 * cells * chans, transcendentals=0
        ),
        name="conv_final" if final else "conv_first",
    )(*operands)
    return out[0] if final else out


def along(x, axis, by):
    size = lax.axis_size(axis)
    return lax.ppermute(x, axis, [(i, i + by) for i in range(size) if 0 <= i + by < size])


def side_flags():
    at, size = lax.axis_index("col"), lax.axis_size("col")
    return jnp.stack([at > 0, at < size - 1]).astype(F32)


def row_parity():
    return (1 - lax.axis_index("row") % 2).astype(jnp.int32)


def row_swaps(below, above):
    size = lax.axis_size("row")
    even = row_parity() == 1
    got = []
    for start, mine in ((0, jnp.where(even, below, above)), (1, jnp.where(even, above, below))):
        pairs = [(i, i + 1) for i in range(start, size - 1, 2)]
        got.append(lax.ppermute(mine, "row", pairs + [(b, a) for a, b in pairs]))
    return got


def exchange(first_row, last_row, first_col, last_col):
    n, cols, chans = first_row.shape
    if lax.axis_size("col") == 2:
        mine = jnp.where(lax.axis_index("col") == 0, last_col, first_col)
        left = right = lax.ppermute(mine, "col", [(0, 1), (1, 0)])
    else:
        left = along(last_col, "col", 1)
        right = along(first_col, "col", -1)
    extra = -(-2 * n // cols)

    def payload(row, at):
        corners = jnp.stack([left[:, at], right[:, at]], axis=1).reshape(2 * n, chans)
        corners = jnp.pad(corners, ((0, extra * cols - 2 * n), (0, 0)))
        return jnp.concatenate([row, corners.reshape(extra, cols, chans)], axis=0)

    below, above = payload(last_row, -1), payload(first_row, 0)
    return *row_swaps(below, above), left, right


def from_earlier(tail, halo):
    top, bottom, left, right = halo
    n, _, chans = left.shape
    parts = [top[n - 2 : n], bottom[n - 2 : n], left[-2:], right[-2:]]
    for part in (top, bottom):
        parts.append(part[n:].reshape(-1, chans)[2 * n - 4 : 2 * n].reshape(2, 2, chans))
    parts.append(jnp.zeros((2, SUB - 4, chans), BF16))
    return along(tail, "ta", 1), along(jnp.concatenate(parts, axis=1), "ta", 1)


def shards(latent_in, norm_gains, conv_weights, conv_bias):
    frames, rows, width, chans = latent_in.shape
    pad = -width % SUB
    x = jnp.pad(latent_in, ((0, 0), (0, 0), (0, pad), (0, 0))) if pad else latent_in
    flags = side_flags()
    late = frames // 2
    last = frames // 4

    tiles, *border, tail = prepare(x, norm_gains[0:1], width)
    halo = exchange(*border)
    early = from_earlier(tail, halo)
    first = dict(flags=flags, parity=row_parity()[None], weights=conv_weights, bias=conv_bias[0:1], gain=norm_gains[1:2],
                 layer=0, rows=rows, width=width)
    second = dict(first, bias=conv_bias[1:2], layer=1, x=x)

    own = (tiles, *halo)
    tiles_b, *border_b, tail = conv([("own", own, late - 2, frames - late + 2)], **first)
    own_b = (tiles_b, *exchange(*border_b))
    tiles_a, *border_a, _ = conv([("rec", early, 0, 2), ("own", own, 0, late)], **first)
    early = from_earlier(tail, own_b[1:])
    own_a = (tiles_a, *exchange(*border_a))
    cut = frames - late - last
    out = conv([("own", own_b, cut - 2, last + 2)], **second, x_start=frames - last)
    out = conv(
        [("rec", early, 0, 2), ("own", own_a, 0, late), ("own", own_b, 0, cut)],
        **second, x_start=0, into=out,
    )
    return out[:, :, :width] if pad else out


def solution(mesh):
    placed = (P("ta", "row", "col", None), P(), P(), P())
    return jax.shard_map(
        shards, mesh=mesh, in_specs=placed, out_specs=P("ta", "row", "col", None), check_vma=False
    )
```

time: 705 us -> 212 us (0.30); the launches traced: 697 us -> 211 us
  matrix products: 426 us -> 0 us
  Pallas kernels: 0 us -> 162 us
  local copies, waits for them, and re-layouts: 144 us -> 7.22 us
  other arithmetic: 53.3 us -> 5.87 us
  waiting for transfers between devices: 47.8 us -> 6.73 us
    dot_general x54 -> x0, matrix products: 426 us -> none  [convolve(): jnp.dot(piece, weight[tap_t, tap_r, tap_c], preferred_element_type=jnp.fl...]
    pallas_call x0 -> x5, Pallas kernels: none -> 162 us  [the longest x4 148 us: conv(): pl.pallas_call(lambda *refs: conv_kernel(cfg, *refs), out_shape=out_shape...]
    slice x12 -> x15, local copies, waits for them, and re-layouts: 89.1 us -> 3.65 us  [the longest x6 1.62 us: from_earlier(): part[n:].reshape(-1, chans)[2 * n - 4:2 * n].reshape(2, 2, chans)]
    reshape x4 -> x14, local copies, waits for them, and re-layouts: 48.5 us -> 0.17 us  [the longest x6 0.09 us: payload(): jnp.stack([left[:, at], right[:, at]], axis=1).reshape(2 * n, chans)]
    ppermute x10 -> x13, waiting for transfers between devices: 47.8 us -> 6.73 us  [the longest x6 6.71 us: row_swaps(): got.append(lax.ppermute(mine, 'row', pairs + [(b, a) for a, b in pairs]))]
    concatenate x2 -> x0, other arithmetic: 21.4 us -> none  [padded_2(): jnp.concatenate([lax.ppermute(tail, axis, [(i, (i + 1) % count) for i in...]
    add x1 -> x0, other arithmetic: 11.3 us -> none  [shards(): return latent_in + second]
    reduce_sum x2 -> x0, other arithmetic: 9.56 us -> none  [activate(): mean_sq = jnp.mean(value * value, axis=-1, keepdims=True)]
  transfers between devices with their start and end apart: 10 -> 13, of which waited for: 8 -> 1; matrix products, arithmetic and copies ran while one was open for 1% -> 4% of each run, Pallas kernels for 0% -> 46%
where the time goes in v1:
time: 212 us; the launch traced here: 211 us
  Pallas kernels  162 us (76%)
  starting transfers between devices  28.4 us (13%)
  local copies, waits for them, and re-layouts  7.22 us (3%)
  waiting for transfers between devices  6.73 us (3%)
  other arithmetic  5.87 us (3%)
    pallas_call x4, Pallas kernels, conv(): pl.pallas_call(lambda *refs: conv_kernel(cfg, *refs), out_shape=out_shape...  148 us
    ppermute x4, starting transfers between devices, along(): lax.ppermute(x, axis, [(i, i + by) for i in range(size) if 0 <= i + by <...  14.8 us
    pallas_call x1, Pallas kernels, prepare(): pl.pallas_call(lambda *refs: prepare_kernel((width - 1) % SUB, *refs), ou...  13.9 us
    ppermute x6, starting transfers between devices, row_swaps(): got.append(lax.ppermute(mine, 'row', pairs + [(b, a) for a, b in pairs]))  12.9 us
    ppermute x6, waiting for transfers between devices, row_swaps(): got.append(lax.ppermute(mine, 'row', pairs + [(b, a) for a, b in pairs]))  6.71 us
  transfers between devices with their start and end apart: 13, of which 1 were waited for; matrix products, arithmetic and copies ran while one was open for 4% of the time, Pallas kernels for 46%

profile of v1, /device:TPU:0, one launch (start us, length us, event | category | flops | bytes accessed | tf_op | source)
XLA Modules:
  0.0 211.1 jit_solution(153051674037225579)
XLA Ops:
  0.0 1.3 fusion.6
  1.3 13.9 %prepare.1 = (bf16[16,384,384]{2,1,0:T(8,128)(2,1)}, bf16[16,24,384]{2,1,0:T(8,128)(2,1)}, bf16[16,24,384]{2,1,0:T(8,128)(2,1)}, bf16[16,16,384]{2,1,0:T(8,128)(...) custom-call(f32[16,16,24,384]{3,2,1,0:T(8,128)} %refs_15_.1, f32[1,384]{1,0:T(1,128)} %get-tuple-element.58.refs_1_), custom_call_target="tpu_custom_call" | custom-call | flops 47185920 | bytes 14155776 | tf_op jit(solution)/shard_map/prepare/pallas_call | solution.py:64
  15.2 1.0 broadcast_select_fusion.2
  16.8 4.4 %collective-permute-start.8 = (bf16[2,384,384]{2,1,0:T(8,128)(2,1)}, bf16[2,384,384]{2,1,0:T(8,128)(2,1)S(1)}, u32[]{:S(2)}, u32[]{:S(2)}) collective-permute-start(bf16[2,384,384]{2,1,0:T(8,128)(2,1)} %get-tuple-element.32), channel_id=1, source_target_pairs={{0,8},{8,16},{16,24},{1,9},{9,17},{17,25},{2,10},{10,18},{18,26},{... | collective-permute-start | bytes 1769480 | tf_op jit(solution)/shard_map/ppermute | solution.py:494
  21.5 1.1 broadcast_select_fusion
  22.6 0.7 collective-permute-start.2
  23.3 4.4 %collective-permute-start.1 = (bf16[18,24,384]{2,1,0:T(8,128)(2,1)S(1)}, bf16[18,24,384]{2,1,0:T(8,128)(2,1)S(1)}, u32[]{:S(2)}, u32[]{:S(2)}) collective-permute-start(bf16[18,24,384]{2,1,0:T(8,128)(2,1)S(1)} %get-tuple-element.40), channel_id=1, source_target_pairs={{0,2},{4,6},{2,0},{6,4},{1,3},{5,7},{3,1},{7,5},{8,10},{12,14},{10... | collective-permute-start | bytes 995336 | tf_op jit(solution)/shard_map/ppermute | solution.py:512
  29.0 6.7 %collective-permute-done.1.refs_1_.refs_3_ = bf16[18,24,384]{2,1,0:T(8,128)(2,1)S(1)} collective-permute-done((bf16[18,24,384]{2,1,0:T(8,128)(2,1)S(1)}, bf16[18,24,384]{2,1,0:T(8,128)(2,1)S(1)}, u32[]{:S(2)}, u32[]{:S(2)}) %collective-permute-start.1) | collective-permute-done | bytes 331808 | tf_op jit(solution)/shard_map/ppermute | solution.py:512
  35.7 0.7 copy-done.5
  36.4 37.3 %conv_first.2 = (bf16[8,384,384]{2,1,0:T(8,128)(2,1)}, bf16[8,24,384]{2,1,0:T(8,128)(2,1)}, bf16[8,24,384]{2,1,0:T(8,128)(2,1)}, bf16[8,16,384]{2,1,0:T(8,128)(2...) custom-call(bf16[16,384,384]{2,1,0:T(8,128)(2,1)} %get-tuple-element.22.refs_0_.refs_2_, ...), custom_call_target="tpu_custom_call" | custom-call | flops 24461180928 | bytes 9437184 | tf_op jit(solution)/shard_map/conv_first/pallas_call | solution.py:469
  73.7 0.9 broadcast_select_fusion.8
  74.7 0.8 fusion
  75.5 0.8 fusion.1
  76.4 3.4 %collective-permute-start.9 = (bf16[2,88,384]{2,1,0:T(8,128)(2,1)S(1)}, bf16[2,88,384]{2,1,0:T(8,128)(2,1)S(1)}, u32[]{:S(2)}, u32[]{:S(2)}) collective-permute-start(bf16[2,88,384]{2,1,0:T(8,128)(2,1)S(1)} %concatenate.29), channel_id=1, source_target_pairs={{0,8},{8,16},{16,24},{1,9},{9,17},{17,25},{2,10},{10,18},{18,26},{... | collective-permute-start | bytes 405512 | tf_op jit(solution)/shard_map/ppermute | solution.py:494
  79.8 3.6 %collective-permute-start.3 = (bf16[2,384,384]{2,1,0:T(8,128)(2,1)}, bf16[2,384,384]{2,1,0:T(8,128)(2,1)S(1)}, u32[]{:S(2)}, u32[]{:S(2)}) collective-permute-start(bf16[2,384,384]{2,1,0:T(8,128)(2,1)} %get-tuple-element.27), channel_id=1, source_target_pairs={{0,8},{8,16},{16,24},{1,9},{9,17},{17,25},{2,10},{10,18},{18,26},{... | collective-permute-start | bytes 1769480 | tf_op jit(solution)/shard_map/ppermute | solution.py:494
  83.7 0.8 copy-done.10
  85.1 37.3 %conv_first.3 = (bf16[8,384,384]{2,1,0:T(8,128)(2,1)}, bf16[8,24,384]{2,1,0:T(8,128)(2,1)}, bf16[8,24,384]{2,1,0:T(8,128)(2,1)}, bf16[8,16,384]{2,1,0:T(8,128)(2...) custom-call(bf16[2,384,384]{2,1,0:T(8,128)(2,1)} %copy-done.10, bf16[2,88,384]{2,1,0:T(8,128)(2,1)} %copy-done.14, ...), custom_call_target="tpu_custom_call" | custom-call | flops 24461180928 | bytes 9437184 | tf_op jit(solution)/shard_map/conv_first/pallas_call | solution.py:469
  122.5 0.9 broadcast_select_fusion.7
  124.2 3.5 %collective-permute-start.5 = (bf16[9,24,384]{2,1,0:T(8,128)(2,1)S(1)}, bf16[9,24,384]{2,1,0:T(8,128)(2,1)S(1)}, u32[]{:S(2)}, u32[]{:S(2)}) collective-permute-start(bf16[9,24,384]{2,1,0:T(8,128)(2,1)S(1)} %get-tuple-element.48), channel_id=1, source_target_pairs={{0,2},{4,6},{2,0},{6,4},{1,3},{5,7},{3,1},{7,5},{8,10},{12,14},{10... | collective-permute-start | bytes 497672 | tf_op jit(solution)/shard_map/ppermute | solution.py:512
  127.9 1.0 broadcast_select_fusion.3
  129.6 2.9 %collective-permute-start.11 = (bf16[9,24,384]{2,1,0:T(8,128)(2,1)S(1)}, bf16[9,24,384]{2,1,0:T(8,128)(2,1)S(1)}, u32[]{:S(2)}, u32[]{:S(2)}) collective-permute-start(bf16[9,24,384]{2,1,0:T(8,128)(2,1)S(1)} %get-tuple-element.42), channel_id=1, source_target_pairs={{0,2},{4,6},{2,0},{6,4},{1,3},{5,7},{3,1},{7,5},{8,10},{12,14},{10... | collective-permute-start | bytes 497672 | tf_op jit(solution)/shard_map/ppermute | solution.py:512
  132.8 3.4 %collective-permute-start.7 = (bf16[2,88,384]{2,1,0:T(8,128)(2,1)S(1)}, bf16[2,88,384]{2,1,0:T(8,128)(2,1)S(1)}, u32[]{:S(2)}, u32[]{:S(2)}) collective-permute-start(bf16[2,88,384]{2,1,0:T(8,128)(2,1)S(1)} %concatenate.28), channel_id=1, source_target_pairs={{0,8},{8,16},{16,24},{1,9},{9,17},{17,25},{2,10},{10,18},{18,26},{... | collective-permute-start | bytes 405512 | tf_op jit(solution)/shard_map/ppermute | solution.py:494
  136.2 21.5 %conv_final.2.refs_16_ = f32[16,16,24,384]{3,2,1,0:T(8,128)} custom-call(bf16[8,384,384]{2,1,0:T(8,128)(2,1)} %get-tuple-element.38.refs_0_.refs_6_, bf16[9,24,384]{2,1,0:T(8,128)(2,1)} %copy-done.7, bf16[9,24,384]{2,1,0:T(8,128)(2,1)} %copy-done.6, bf16[8,16,384]{2,1,0:T(8,128)(2,1)} %copy-done.3, f32[2]{0:T(128)} %add_convert_fusion.refs_4_.refs_6_.refs_10_, ...), custom_call_target="tpu_custom_call" | custom-call | flops 12230590464 | bytes 4718592 | tf_op jit(solution)/shard_map/conv_final/pallas_call | solution.py:469
  158.8 52.1 %conv_final.3 = f32[16,16,24,384]{3,2,1,0:T(8,128)} custom-call(bf16[2,384,384]{2,1,0:T(8,128)(2,1)} %copy-done.11, bf16[2,88,384]{2,1,0:T(8,128)(2,1)} %copy-done.15, bf16[8,384,384]{2,1,0:T(8,128)(2,1)} %get-tuple-element.33.refs_2_, bf16[9,24,384]{2,1,0:T(8,128)(2,1)} %copy-done.13, ...), custom_call_target="tpu_custom_call", output_to_operand_aliasing={{}: (16, {})} | custom-call | flops 36691771392 | bytes 14155776 | tf_op jit(solution)/shard_map/conv_final/pallas_call | solution.py:469
  (85 shorter events, 5.7 us)
Async XLA Ops:
  0.0 28.4 %copy-start.9 = (f32[2,384]{1,0:T(2,128)S(1)}, f32[2,384]{1,0:T(2,128)}, u32[]{:S(2)}) copy-start(f32[2,384]{1,0:T(2,128)} %param.7) | copy-start | bytes 9220
  16.2 5.0 %collective-permute-start = (bf16[16,16,384]{2,1,0:T(8,128)(2,1)S(1)}, bf16[16,16,384]{2,1,0:T(8,128)(2,1)S(1)}, u32[]{:S(2)}, u32[]{:S(2)}) collective-permute-start(bf16[16,16,384]{2,1,0:T(8,128)(2,1)S(1)} %broadcast_select_fusion.2), channel_id=1, source_target_pairs={{0,1},{1,0},{2,3},{3,2},{4,5},{5,4},{6,7},{7,6},{8,9},{9,8},{10,11... | collective-permute-start | bytes 589832 | tf_op jit(solution)/shard_map/ppermute | solution.py:520
  16.8 66.9 %collective-permute-start.8 = (bf16[2,384,384]{2,1,0:T(8,128)(2,1)}, bf16[2,384,384]{2,1,0:T(8,128)(2,1)S(1)}, u32[]{:S(2)}, u32[]{:S(2)}) collective-permute-start(bf16[2,384,384]{2,1,0:T(8,128)(2,1)} %get-tuple-element.32), channel_id=1, source_target_pairs={{0,8},{8,16},{16,24},{1,9},{9,17},{17,25},{2,10},{10,18},{18,26},{... | collective-permute-start | bytes 1769480 | tf_op jit(solution)/shard_map/ppermute | solution.py:494
  21.2 14.4 %copy-start.2 = (bf16[16,16,384]{2,1,0:T(8,128)(2,1)}, bf16[16,16,384]{2,1,0:T(8,128)(2,1)S(1)}, u32[]{:S(2)}) copy-start(bf16[16,16,384]{2,1,0:T(8,128)(2,1)S(1)} %collective-permute-done.refs_3_.refs_5_) | copy-start | bytes 589828
  22.6 6.3 %collective-permute-start.2 = (bf16[18,24,384]{2,1,0:T(8,128)(2,1)S(1)}, bf16[18,24,384]{2,1,0:T(8,128)(2,1)S(1)}, u32[]{:S(2)}, u32[]{:S(2)}) collective-permute-start(bf16[18,24,384]{2,1,0:T(8,128)(2,1)S(1)} %get-tuple-element.39), channel_id=1, source_target_pairs={{2,4},{4,2},{3,5},{5,3},{10,12},{12,10},{11,13},{13,11},{18,20},{2... | collective-permute-start | bytes 995336 | tf_op jit(solution)/shard_map/ppermute | solution.py:512
  23.3 12.3 %collective-permute-start.1 = (bf16[18,24,384]{2,1,0:T(8,128)(2,1)S(1)}, bf16[18,24,384]{2,1,0:T(8,128)(2,1)S(1)}, u32[]{:S(2)}, u32[]{:S(2)}) collective-permute-start(bf16[18,24,384]{2,1,0:T(8,128)(2,1)S(1)} %get-tuple-element.40), channel_id=1, source_target_pairs={{0,2},{4,6},{2,0},{6,4},{1,3},{5,7},{3,1},{7,5},{8,10},{12,14},{10... | collective-permute-start | bytes 995336 | tf_op jit(solution)/shard_map/ppermute | solution.py:512
  28.9 6.7 %copy-start.4 = (bf16[18,24,384]{2,1,0:T(8,128)(2,1)}, bf16[18,24,384]{2,1,0:T(8,128)(2,1)S(1)}, u32[]{:S(2)}) copy-start(bf16[18,24,384]{2,1,0:T(8,128)(2,1)S(1)} %collective-permute-done.2.refs_2_.refs_4_) | copy-start | bytes 995332
  74.6 8.8 %collective-permute-start.4 = (bf16[8,16,384]{2,1,0:T(8,128)(2,1)S(1)}, bf16[8,16,384]{2,1,0:T(8,128)(2,1)S(1)}, u32[]{:S(2)}, u32[]{:S(2)}) collective-permute-start(bf16[8,16,384]{2,1,0:T(8,128)(2,1)S(1)} %broadcast_select_fusion.8), channel_id=1, source_target_pairs={{0,1},{1,0},{2,3},{3,2},{4,5},{5,4},{6,7},{7,6},{8,9},{9,8},{10,11... | collective-permute-start | bytes 294920 | tf_op jit(solution)/shard_map/ppermute | solution.py:520
  76.4 7.2 %collective-permute-start.9 = (bf16[2,88,384]{2,1,0:T(8,128)(2,1)S(1)}, bf16[2,88,384]{2,1,0:T(8,128)(2,1)S(1)}, u32[]{:S(2)}, u32[]{:S(2)}) collective-permute-start(bf16[2,88,384]{2,1,0:T(8,128)(2,1)S(1)} %concatenate.29), channel_id=1, source_target_pairs={{0,8},{8,16},{16,24},{1,9},{9,17},{17,25},{2,10},{10,18},{18,26},{... | collective-permute-start | bytes 405512 | tf_op jit(solution)/shard_map/ppermute | solution.py:494
  79.8 78.0 %collective-permute-start.3 = (bf16[2,384,384]{2,1,0:T(8,128)(2,1)}, bf16[2,384,384]{2,1,0:T(8,128)(2,1)S(1)}, u32[]{:S(2)}, u32[]{:S(2)}) collective-permute-start(bf16[2,384,384]{2,1,0:T(8,128)(2,1)} %get-tuple-element.27), channel_id=1, source_target_pairs={{0,8},{8,16},{16,24},{1,9},{9,17},{17,25},{2,10},{10,18},{18,26},{... | collective-permute-start | bytes 1769480 | tf_op jit(solution)/shard_map/ppermute | solution.py:494
  83.4 44.3 %copy-start.3 = (bf16[8,16,384]{2,1,0:T(8,128)(2,1)}, bf16[8,16,384]{2,1,0:T(8,128)(2,1)S(1)}, u32[]{:S(2)}) copy-start(bf16[8,16,384]{2,1,0:T(8,128)(2,1)S(1)} %collective-permute-done.4.refs_3_.refs_9_) | copy-start | bytes 294916
  83.6 39.9 %copy-start = (bf16[8,24,384]{2,1,0:T(8,128)(2,1)S(1)}, bf16[8,24,384]{2,1,0:T(8,128)(2,1)}, u32[]{:S(2)}) copy-start(bf16[8,24,384]{2,1,0:T(8,128)(2,1)} %get-tuple-element.31) | copy-start | bytes 442372
  83.6 39.9 %copy-start.1 = (bf16[8,24,384]{2,1,0:T(8,128)(2,1)S(1)}, bf16[8,24,384]{2,1,0:T(8,128)(2,1)}, u32[]{:S(2)}) copy-start(bf16[8,24,384]{2,1,0:T(8,128)(2,1)} %get-tuple-element.28) | copy-start | bytes 442372
  83.6 0.8 copy-start.10
  123.4 4.3 %collective-permute-start.10 = (bf16[8,16,384]{2,1,0:T(8,128)(2,1)S(1)}, bf16[8,16,384]{2,1,0:T(8,128)(2,1)S(1)}, u32[]{:S(2)}, u32[]{:S(2)}) collective-permute-start(bf16[8,16,384]{2,1,0:T(8,128)(2,1)S(1)} %broadcast_select_fusion.7), channel_id=1, source_target_pairs={{0,1},{1,0},{2,3},{3,2},{4,5},{5,4},{6,7},{7,6},{8,9},{9,8},{10,11... | collective-permute-start | bytes 294920 | tf_op jit(solution)/shard_map/ppermute | solution.py:520
  123.6 9.0 %collective-permute-start.6 = (bf16[9,24,384]{2,1,0:T(8,128)(2,1)S(1)}, bf16[9,24,384]{2,1,0:T(8,128)(2,1)S(1)}, u32[]{:S(2)}, u32[]{:S(2)}) collective-permute-start(bf16[9,24,384]{2,1,0:T(8,128)(2,1)S(1)} %get-tuple-element.47), channel_id=1, source_target_pairs={{2,4},{4,2},{3,5},{5,3},{10,12},{12,10},{11,13},{13,11},{18,20},{2... | collective-permute-start | bytes 497672 | tf_op jit(solution)/shard_map/ppermute | solution.py:512
  124.2 8.4 %collective-permute-start.5 = (bf16[9,24,384]{2,1,0:T(8,128)(2,1)S(1)}, bf16[9,24,384]{2,1,0:T(8,128)(2,1)S(1)}, u32[]{:S(2)}, u32[]{:S(2)}) collective-permute-start(bf16[9,24,384]{2,1,0:T(8,128)(2,1)S(1)} %get-tuple-element.48), channel_id=1, source_target_pairs={{0,2},{4,6},{2,0},{6,4},{1,3},{5,7},{3,1},{7,5},{8,10},{12,14},{10... | collective-permute-start | bytes 497672 | tf_op jit(solution)/shard_map/ppermute | solution.py:512
  127.7 30.0 %copy-start.8 = (bf16[8,16,384]{2,1,0:T(8,128)(2,1)}, bf16[8,16,384]{2,1,0:T(8,128)(2,1)S(1)}, u32[]{:S(2)}) copy-start(bf16[8,16,384]{2,1,0:T(8,128)(2,1)S(1)} %collective-permute-done.10.refs_5_) | copy-start | bytes 294916
  129.0 28.8 %collective-permute-start.12 = (bf16[9,24,384]{2,1,0:T(8,128)(2,1)S(1)}, bf16[9,24,384]{2,1,0:T(8,128)(2,1)S(1)}, u32[]{:S(2)}, u32[]{:S(2)}) collective-permute-start(bf16[9,24,384]{2,1,0:T(8,128)(2,1)S(1)} %get-tuple-element.41), channel_id=1, source_target_pairs={{2,4},{4,2},{3,5},{5,3},{10,12},{12,10},{11,13},{13,11},{18,20},{2... | collective-permute-start | bytes 497672 | tf_op jit(solution)/shard_map/ppermute | solution.py:512
  129.6 28.1 %collective-permute-start.11 = (bf16[9,24,384]{2,1,0:T(8,128)(2,1)S(1)}, bf16[9,24,384]{2,1,0:T(8,128)(2,1)S(1)}, u32[]{:S(2)}, u32[]{:S(2)}) collective-permute-start(bf16[9,24,384]{2,1,0:T(8,128)(2,1)S(1)} %get-tuple-element.42), channel_id=1, source_target_pairs={{0,2},{4,6},{2,0},{6,4},{1,3},{5,7},{3,1},{7,5},{8,10},{12,14},{10... | collective-permute-start | bytes 497672 | tf_op jit(solution)/shard_map/ppermute | solution.py:512
  132.6 3.6 %copy-start.6 = (bf16[9,24,384]{2,1,0:T(8,128)(2,1)}, bf16[9,24,384]{2,1,0:T(8,128)(2,1)S(1)}, u32[]{:S(2)}) copy-start(bf16[9,24,384]{2,1,0:T(8,128)(2,1)S(1)} %collective-permute-done.6.refs_2_.refs_8_) | copy-start | bytes 497668
  132.6 3.6 %copy-start.7 = (bf16[9,24,384]{2,1,0:T(8,128)(2,1)}, bf16[9,24,384]{2,1,0:T(8,128)(2,1)S(1)}, u32[]{:S(2)}) copy-start(bf16[9,24,384]{2,1,0:T(8,128)(2,1)S(1)} %collective-permute-done.5.refs_1_.refs_7_) | copy-start | bytes 497668
  132.8 25.0 %collective-permute-start.7 = (bf16[2,88,384]{2,1,0:T(8,128)(2,1)S(1)}, bf16[2,88,384]{2,1,0:T(8,128)(2,1)S(1)}, u32[]{:S(2)}, u32[]{:S(2)}) collective-permute-start(bf16[2,88,384]{2,1,0:T(8,128)(2,1)S(1)} %concatenate.28), channel_id=1, source_target_pairs={{0,8},{8,16},{16,24},{1,9},{9,17},{17,25},{2,10},{10,18},{18,26},{... | collective-permute-start | bytes 405512 | tf_op jit(solution)/shard_map/ppermute | solution.py:494
  157.8 0.9 copy-start.11
  (5 other events, 3.5 us)

commit v2 on v1

--- a/solution.py
+++ b/solution.py
@@ -6,7 +6,6 @@
 from jax.sharding import PartitionSpec as P
 
 EPS = 1e-06
-PARITY = True
 SUB = 8
 LANE = 128
 F32 = jnp.float32
@@ -34,49 +33,69 @@
     return parts
 
 
-def prepare_kernel(last_valid, x_ref, gain_ref, out_ref, row0, row1, col0, col1, tail_ref, row_f, col_f):
+def prepare_kernel(last_valid, total, x_ref, gain_ref, pick_ref, out_ref, row0, row1, col0, col1, tail_ref, row_f, col_f):
     half, blocks = x_ref.shape[1] // 2, x_ref.shape[2] // SUB
+    count = x_ref.shape[0]
     gain = gain_ref[...]
-    for r in range(half):
-        for j in range(blocks):
-            cols = pl.ds(j * SUB, SUB)
-            v = jnp.concatenate([x_ref[0, r, cols, :], x_ref[0, r + half, cols, :]], axis=0)
-            a = activate(v, gain)
-            out_ref[0, pl.ds((r * blocks + j) * 16, 16), :] = a
-            tail_ref[0, pl.ds((r * blocks + j) * 16, 16), :] = a
-            for kind, e, row, piece in border_parts(a.astype(F32), r, j, half, blocks, last_valid):
-                dst = row_f if kind == "row" else col_f
-                dst[e, pl.ds(row, piece.shape[0]), :] = piece
-    row0[0] = row_f[0].astype(BF16)
-    row1[0] = row_f[1].astype(BF16)
-    col0[0] = col_f[0].astype(BF16)
-    col1[0] = col_f[1].astype(BF16)
-
-
-def prepare(x, gain, width):
+    even, side = pick_ref[0], pick_ref[1]
+
+    def frame(k, carry):
+        kept = jnp.maximum(pl.program_id(0) * count + k - (total - 2), 0)
+        for r in range(half):
+            for j in range(blocks):
+                cols = pl.ds(j * SUB, SUB)
+                v = jnp.concatenate([x_ref[k, r, cols, :], x_ref[k, r + half, cols, :]], axis=0)
+                a = activate(v, gain)
+                here = pl.ds((r * blocks + j) * 16, 16)
+                out_ref[k, here, :] = a
+                tail_ref[kept, here, :] = a
+                for kind, e, row, piece in border_parts(a.astype(F32), r, j, half, blocks, last_valid):
+                    dst = row_f if kind == "row" else col_f
+                    dst[e, pl.ds(row, piece.shape[0]), :] = piece
+        row0[k] = row_f[even].astype(BF16)
+        row1[k] = row_f[1 - even].astype(BF16)
+        col0[k] = col_f[side].astype(BF16)
+        col1[k] = col_f[1 - side].astype(BF16)
+        return carry
+
+    lax.fori_loop(0, count, frame, 0)
+
+
+def extra_frames(n, cols):
+    return -(-2 * n // cols)
+
+
+def record_rows(rows, cols):
+    return rows * cols + 2 * (rows + cols) + SUB
+
+
+def prepare(x, gain, picks, width):
     frames, rows, cols, chans = x.shape
     cells = rows * cols
+    step = 4 if frames % 4 == 0 else 1
+    m = extra_frames(frames, cols)
 
     def spec(n):
-        return pl.BlockSpec((1, n, chans), lambda f: (f, 0, 0))
-
-    sizes = (cells, cols, cols, rows, rows)
+        return pl.BlockSpec((step, n, chans), lambda f: (f, 0, 0))
+
+    sizes = ((cells, 0), (cols, m), (cols, m), (rows, 0), (rows, 0))
+    keep = (2, record_rows(rows, cols), chans)
     return pl.pallas_call(
-        lambda *refs: prepare_kernel((width - 1) % SUB, *refs),
-        out_shape=[jax.ShapeDtypeStruct((frames, n, chans), BF16) for n in sizes]
-        + [jax.ShapeDtypeStruct((2, cells, chans), BF16)],
-        grid=(frames,),
+        lambda *refs: prepare_kernel((width - 1) % SUB, frames, *refs),
+        out_shape=[jax.ShapeDtypeStruct((frames + more, n, chans), BF16) for n, more in sizes]
+        + [jax.ShapeDtypeStruct(keep, BF16)],
+        grid=(frames // step,),
         in_specs=[
-            pl.BlockSpec((1, rows, cols, chans), lambda f: (f, 0, 0, 0)),
+            pl.BlockSpec((step, rows, cols, chans), lambda f: (f, 0, 0, 0)),
             pl.BlockSpec((1, chans), lambda f: (0, 0)),
+            pl.BlockSpec(memory_space=pltpu.SMEM),
         ],
-        out_specs=[spec(n) for n in sizes]
-        + [pl.BlockSpec((1, cells, chans), lambda f: (jnp.maximum(f - (frames - 2), 0), 0, 0))],
+        out_specs=[spec(n) for n, _ in sizes] + [pl.BlockSpec(keep, lambda f: (0, 0, 0))],
         scratch_shapes=[pltpu.VMEM((2, cols, chans), F32), pltpu.VMEM((2, rows, chans), F32)],
         compiler_params=pltpu.CompilerParams(vmem_limit_bytes=60 << 20),
         cost_estimate=pl.CostEstimate(flops=20 * x.size, bytes_accessed=6 * x.size, transcendentals=2 * x.size),
         name="prepare",
-    )(x, gain)
+    )(x, gain, picks)
 
 
 def conv_kernel(cfg, *refs):
@@ -89,7 +108,7 @@
     n_chunk = chans // LANE
     ins = refs[:n_ops]
     at = n_ops
-    flag_ref, parity_ref, w_hbm, bias_ref, gain_ref = refs[at : at + 5]
+    flag_ref, pick_ref, w_hbm, bias_ref, gain_ref = refs[at : at + 5]
     at += 5
     if final:
         x_hbm = refs[at]
@@ -102,7 +121,8 @@
     (a_buf, w_buf, t_buf, edge_buf, side_buf, corner_buf, edge_f, side_f, corner_f, pm, p3, o_buf,
      row_f, col_f, row_buf, col_buf, in_sem, w_sem, x_sem, o_sem, b_sem) = refs[at:]
     taps = [(dt, dr, dc) for dt in range(3) for dr in range(3) for dc in range(3)]
-    slots = (parity_ref[0], 1 - parity_ref[0])
+    even, side = pick_ref[0], pick_ref[1]
+    slots = (even, 1 - even)
 
     copies = []
 
@@ -112,6 +132,7 @@
     base = 0
     corner_at = 0
     corners = []
+    earlier = []
     for kind, which, start, count in segs:
         here = pl.ds(base, count)
         if kind == "own":
@@ -128,12 +149,15 @@
                 fetch(part.at[there], side_buf.at[e, here])
             corner_at += extra
         else:
-            t, rec = [ins[n] for n in which]
-            fetch(t, t_buf.at[here])
+            (rec,) = [ins[n] for n in which]
+            off = rows * cols
+            fetch(rec.at[:, pl.ds(0, off)], t_buf.at[here])
             for e in range(2):
-                fetch(rec.at[:, pl.ds(e * cols, cols)], edge_buf.at[e, here])
-                fetch(rec.at[:, pl.ds(2 * cols + e * rows, rows)], side_buf.at[e, here])
-            fetch(rec.at[:, pl.ds(2 * (cols + rows), SUB)], corner_buf.at[0, pl.ds(corner_at, count), pl.ds(0, SUB)])
+                fetch(rec.at[:, pl.ds(off + e * cols, cols)], edge_buf.at[e, here])
+                fetch(rec.at[:, pl.ds(off + 2 * cols + e * rows, rows)], side_buf.at[e, here])
+            off += 2 * (cols + rows)
+            fetch(rec.at[:, pl.ds(off, SUB)], corner_buf.at[0, pl.ds(corner_at, count), pl.ds(0, SUB)])
+            earlier.append((here, pl.ds(corner_at, count)))
             for e in range(2):
                 for k in range(count):
                     corners.append((e, 0, corner_at + k, 1, 2 * e, base + k, 1))
@@ -148,24 +172,31 @@
     ]
     for c in copies:
         c.start()
+    for c in copies:
+        c.wait()
     for c in w_copies:
         c.start()
-    if final:
-        x_copy = pltpu.make_async_copy(x_hbm.at[pl.ds(x_start, n_out)], o_buf, x_sem)
-        x_copy.start()
-    for c in copies:
-        c.wait()
+
+    for here, corner_here in earlier:
+
+        @pl.when(pick_ref[2] == 0)
+        def _():
+            t_buf[here] = jnp.zeros((2, rows * cols, chans), BF16)
+            for e in range(2):
+                edge_buf[e, here] = jnp.zeros((2, cols, chans), BF16)
+                side_buf[e, here] = jnp.zeros((2, rows, chans), BF16)
+            corner_buf[0, corner_here] = jnp.zeros((2, cols, chans), BF16)
 
     def widen(f, carry):
         for e in range(2):
-            edge_f[e, f] = edge_buf[e, f].astype(F32)
+            edge_f[e, f] = edge_buf[e, f].astype(F32) * flag_ref[2 + e]
             side_f[e, f] = side_buf[e, f].astype(F32) * flag_ref[e]
         return carry
 
     lax.fori_loop(0, n_in, widen, 0)
     for e, source, where, extra, first, base_, count in corners:
         block = corner_buf[source, pl.ds(where, extra)].astype(F32).reshape(extra * cols, chans)
-        corner_f[e, pl.ds(2 * base_, 2 * count), :] = block[first : first + 2 * count]
+        corner_f[e, pl.ds(2 * base_, 2 * count), :] = block[first : first + 2 * count] * flag_ref[2 + e]
 
     sub_index = lax.broadcasted_iota(jnp.int32, (SUB, chans), 0)
     is_first = sub_index == 0
@@ -223,7 +254,7 @@
         for ref, index, value in stores:
             ref[index] = value
 
-    def finish(q, f, r, j, live=None):
+    def finish(q, f, r, j):
         if r == half:
             stores = []
             for e in range(2):
@@ -243,8 +274,6 @@
         for h in range(2):
             index = (f, r + half * h, pl.ds(j * SUB, SUB), slice(None))
             part = v[h * SUB : (h + 1) * SUB]
-            if live is not None:
-                part = jnp.where(live, part, 0.0)
             stores.append((o_buf, index, o_buf[index] + part))
         return stores
 
@@ -330,12 +359,21 @@
         for c in w_copies:
             c.wait()
         if final:
-            x_copy.wait()
+            x_copy = pltpu.make_async_copy(x_hbm.at[pl.ds(x_start, n_out)], o_buf.at[pl.ds(0, n_out)], x_sem)
+            x_copy.start()
+            if steps == 1:
+                x_copy.wait()
 
         def step(i, carry):
             o = 2 * i
-            done = jnp.maximum(o - 2, 0)
-            live = i > 0
+            if final:
+                done = jnp.where(i > 0, o - 2, n_out)
+
+                @pl.when(i == 1)
+                def _():
+                    x_copy.wait()
+            else:
+                done = jnp.maximum(o - 2, 0)
             todo = [(q, r, j) for q in range(2) for r, j in units]
             lead = 3
             pending = []
@@ -351,7 +389,7 @@
                     if r == half:
                         put(pending)
                         pending = []
-                    pending += finish(q, done + q, r, j, live)
+                    pending += finish(q, done + q, r, j)
             put(pending)
 
             new = jnp.minimum(o + 4, n_in - 2)
@@ -386,9 +424,13 @@
         last = [out_copy(steps - 1)]
         if not final:
             for e in range(2):
-                last.append(pltpu.make_async_copy(row_buf.at[e], outs[1 + e], b_sem.at[e]))
-                last.append(pltpu.make_async_copy(col_buf.at[e], outs[3 + e], b_sem.at[2 + e]))
-            last.append(pltpu.make_async_copy(o_buf.at[pl.ds(n_out - 2, 2)], outs[5], b_sem.at[4]))
+                row_from = even if e == 0 else 1 - even
+                col_from = side if e == 0 else 1 - side
+                row_to = outs[1 + e].at[pl.ds(0, n_out)]
+                last.append(pltpu.make_async_copy(row_buf.at[row_from], row_to, b_sem.at[e]))
+                last.append(pltpu.make_async_copy(col_buf.at[col_from], outs[3 + e], b_sem.at[2 + e]))
+            tail_to = outs[5].at[:, pl.ds(0, rows * cols)]
+            last.append(pltpu.make_async_copy(o_buf.at[pl.ds(n_out - 2, 2)], tail_to, b_sem.at[4]))
         for c in last:
             c.start()
         for i in range(steps - 1):
@@ -403,7 +445,7 @@
     )
 
 
-def conv(segments, flags, parity, weights, bias, gain, layer, rows, width, x=None, x_start=0, into=None):
+def conv(segments, flags, picks, weights, bias, gain, layer, rows, width, x=None, x_start=0, into=None):
     blocks = -(-width // SUB)
     cols = blocks * SUB
     chans = weights.shape[-1]
@@ -423,11 +465,12 @@
     n_out = n_in - 2
     half = rows // 2
     wide = blocks * 16
+    m = extra_frames(n_out, cols)
     final = 0 if x is None else (1 if into is None else 2)
     cfg = (tuple(cfg_segs), n_ops, n_in, rows, blocks, chans, layer, (width - 1) % SUB, final, x_start)
     any_spec = pl.BlockSpec(memory_space=pltpu.HBM)
     vmem_spec = pl.BlockSpec(memory_space=pltpu.VMEM)
-    operands += [flags, parity, weights, bias, gain]
+    operands += [flags, picks, weights, bias, gain]
     in_specs = [any_spec] * n_ops + [pl.BlockSpec(memory_space=pltpu.SMEM)] * 2 + [any_spec, vmem_spec, vmem_spec]
     aliases = {}
     if final:
@@ -438,12 +481,13 @@
             operands.append(into)
             in_specs.append(any_spec)
         out_shape = [jax.ShapeDtypeStruct(x.shape, F32)]
-        o_buf = pltpu.VMEM((n_out, rows, cols, chans), F32)
+        o_buf = pltpu.VMEM((n_out + 2, rows, cols, chans), F32)
     else:
         out_shape = [
-            jax.ShapeDtypeStruct((n_out, n, chans), BF16) for n in (rows * cols, cols, cols, rows, rows)
+            jax.ShapeDtypeStruct((n_out + more, n, chans), BF16)
+            for n, more in ((rows * cols, 0), (cols, m), (cols, m), (rows, 0), (rows, 0))
         ]
-        out_shape.append(jax.ShapeDtypeStruct((2, rows * cols, chans), BF16))
+        out_shape.append(jax.ShapeDtypeStruct((2, record_rows(rows, cols), chans), BF16))
         o_buf = pltpu.VMEM((n_out, rows * cols, chans), BF16)
     n_border = 1 if final else n_out
     copies = sum(7 if kind == "own" else 6 for kind, _, _, count in segments)
@@ -494,79 +538,84 @@
     return lax.ppermute(x, axis, [(i, i + by) for i in range(size) if 0 <= i + by < size])
 
 
-def side_flags():
-    at, size = lax.axis_index("col"), lax.axis_size("col")
-    return jnp.stack([at > 0, at < size - 1]).astype(F32)
-
-
-def row_parity():
-    return (1 - lax.axis_index("row") % 2).astype(jnp.int32)
-
-
-def row_swaps(below, above):
+def neighbours():
+    row, col = lax.axis_index("row"), lax.axis_index("col")
+    rows, cols = lax.axis_size("row"), lax.axis_size("col")
+    even = 1 - row % 2
+    second = jnp.where(even == 1, row > 0, row < rows - 1)
+    flags = jnp.stack([col > 0, col < cols - 1, jnp.bool_(True), second]).astype(F32)
+    side = 1 - col if cols == 2 else jnp.zeros_like(col)
+    picks = jnp.stack([even, side, lax.axis_index("ta")]).astype(jnp.int32)
+    return flags, picks
+
+
+def row_swaps(first, second):
     size = lax.axis_size("row")
-    even = row_parity() == 1
     got = []
-    for start, mine in ((0, jnp.where(even, below, above)), (1, jnp.where(even, above, below))):
+    for start, mine in ((0, first), (1, second)):
         pairs = [(i, i + 1) for i in range(start, size - 1, 2)]
         got.append(lax.ppermute(mine, "row", pairs + [(b, a) for a, b in pairs]))
     return got
 
 
-def exchange(first_row, last_row, first_col, last_col):
-    n, cols, chans = first_row.shape
+def exchange(even, row_a, row_b, col_a, col_b):
+    n, _, chans = col_a.shape
+    cols = row_a.shape[1]
     if lax.axis_size("col") == 2:
-        mine = jnp.where(lax.axis_index("col") == 0, last_col, first_col)
-        left = right = lax.ppermute(mine, "col", [(0, 1), (1, 0)])
+        left = right = lax.ppermute(col_a, "col", [(0, 1), (1, 0)])
     else:
-        left = along(last_col, "col", 1)
-        right = along(first_col, "col", -1)
-    extra = -(-2 * n // cols)
-
-    def payload(row, at):
-        corners = jnp.stack([left[:, at], right[:, at]], axis=1).reshape(2 * n, chans)
+        left = along(col_b, "col", 1)
+        right = along(col_a, "col", -1)
+    extra = extra_frames(n, cols)
+
+    def payload(row, last):
+        corners = [jnp.where(last, side[:, -1], side[:, 0]) for side in (left, right)]
+        corners = jnp.stack(corners, axis=1).reshape(2 * n, chans)
         corners = jnp.pad(corners, ((0, extra * cols - 2 * n), (0, 0)))
-        return jnp.concatenate([row, corners.reshape(extra, cols, chans)], axis=0)
-
-    below, above = payload(last_row, -1), payload(first_row, 0)
-    return *row_swaps(below, above), left, right
-
-
-def from_earlier(tail, halo):
-    top, bottom, left, right = halo
+        return lax.dynamic_update_slice(row, corners.reshape(extra, cols, chans), (n, 0, 0))
+
+    rows = payload(row_a, even == 1), payload(row_b, even == 0)
+    return *row_swaps(*rows), left, right
+
+
+def from_earlier(record, halo):
+    a, b, left, right = halo
     n, _, chans = left.shape
-    parts = [top[n - 2 : n], bottom[n - 2 : n], left[-2:], right[-2:]]
-    for part in (top, bottom):
+    parts = [a[n - 2 : n], b[n - 2 : n], left[-2:], right[-2:]]
+    for part in (a, b):
         parts.append(part[n:].reshape(-1, chans)[2 * n - 4 : 2 * n].reshape(2, 2, chans))
     parts.append(jnp.zeros((2, SUB - 4, chans), BF16))
-    return along(tail, "ta", 1), along(jnp.concatenate(parts, axis=1), "ta", 1)
+    packed = jnp.concatenate(parts, axis=1)
+    record = lax.dynamic_update_slice(record, packed, (0, record.shape[1] - packed.shape[1], 0))
+    size = lax.axis_size("ta")
+    return lax.ppermute(record, "ta", [(i, (i + 1) % size) for i in range(size)])
 
 
 def shards(latent_in, norm_gains, conv_weights, conv_bias):
     frames, rows, width, chans = latent_in.shape
     pad = -width % SUB
     x = jnp.pad(latent_in, ((0, 0), (0, 0), (0, pad), (0, 0))) if pad else latent_in
-    flags = side_flags()
+    flags, picks = neighbours()
     late = frames // 2
     last = frames // 4
 
-    tiles, *border, tail = prepare(x, norm_gains[0:1], width)
-    halo = exchange(*border)
+    tiles, *border, tail = prepare(x, norm_gains[0:1], picks, width)
+    halo = exchange(picks[0], *border)
     early = from_earlier(tail, halo)
-    first = dict(flags=flags, parity=row_parity()[None], weights=conv_weights, bias=conv_bias[0:1], gain=norm_gains[1:2],
+    first = dict(flags=flags, picks=picks, weights=conv_weights, bias=conv_bias[0:1], gain=norm_gains[1:2],
                  layer=0, rows=rows, width=width)
     second = dict(first, bias=conv_bias[1:2], layer=1, x=x)
 
     own = (tiles, *halo)
     tiles_b, *border_b, tail = conv([("own", own, late - 2, frames - late + 2)], **first)
-    own_b = (tiles_b, *exchange(*border_b))
-    tiles_a, *border_a, _ = conv([("rec", early, 0, 2), ("own", own, 0, late)], **first)
+    own_b = (tiles_b, *exchange(picks[0], *border_b))
+    tiles_a, *border_a, _ = conv([("rec", (early,), 0, 2), ("own", own, 0, late)], **first)
     early = from_earlier(tail, own_b[1:])
-    own_a = (tiles_a, *exchange(*border_a))
+    own_a = (tiles_a, *exchange(picks[0], *border_a))
     cut = frames - late - last
     out = conv([("own", own_b, cut - 2, last + 2)], **second, x_start=frames - last)
     out = conv(
-        [("rec", early, 0, 2), ("own", own_a, 0, late), ("own", own_b, 0, cut)],
+        [("rec", (early,), 0, 2), ("own", own_a, 0, late), ("own", own_b, 0, cut)],
         **second, x_start=0, into=out,
     )
     return out[:, :, :width] if pad else out

time: 212 us -> 195 us (0.920)
  starting transfers between devices: 28.4 us -> 17.7 us
  Pallas kernels: 162 us -> 156 us
  waiting for transfers between devices: 6.73 us -> 11.1 us
  other arithmetic: 5.87 us -> 1.7 us
    ppermute x7 -> x5, starting transfers between devices: 15.5 us -> 4.39 us  [the longest x2 3.2 us: from_earlier(): lax.ppermute(record, 'ta', [(i, (i + 1) % size) for i in range(size)])]
    select_n x6 -> x2, other arithmetic: 5.03 us -> 0.12 us  [payload(): jnp.where(last, side[:, -1], side[:, 0])]
    pallas_call x1, Pallas kernels: 13.9 us -> 9.64 us  [prepare(): pl.pallas_call(lambda *refs: prepare_kernel((width - 1) % SUB, frames, *r...]
    dynamic_update_slice x0 -> x8, local copies, waits for them, and re-layouts: none -> 3.16 us  [the longest x6 2.46 us: payload(): lax.dynamic_update_slice(row, corners.reshape(extra, cols, chans), (n, 0,...]
    ppermute x6, waiting for transfers between devices: 6.71 us -> 9.3 us  [row_swaps(): got.append(lax.ppermute(mine, 'row', pairs + [(b, a) for a, b in pairs]))]
  transfers between devices with their start and end apart: 13 -> 11, of which waited for: 1 -> 4; matrix products, arithmetic and copies ran while one was open for 4% -> 2% of each run, Pallas kernels for 46% -> 49%
where the time goes in v2:
time: 195 us
  Pallas kernels  156 us (80%)
  starting transfers between devices  17.7 us (9%)
  waiting for transfers between devices  11.1 us (6%)
  local copies, waits for them, and re-layouts  7.41 us (4%)
    pallas_call x4, Pallas kernels, conv(): pl.pallas_call(lambda *refs: conv_kernel(cfg, *refs), out_shape=out_shape...  147 us
    ppermute x6, starting transfers between devices, row_swaps(): got.append(lax.ppermute(mine, 'row', pairs + [(b, a) for a, b in pairs]))  13.3 us
    pallas_call x1, Pallas kernels, prepare(): pl.pallas_call(lambda *refs: prepare_kernel((width - 1) % SUB, frames, *r...  9.64 us
    ppermute x6, waiting for transfers between devices, row_swaps(): got.append(lax.ppermute(mine, 'row', pairs + [(b, a) for a, b in pairs]))  9.3 us
  transfers between devices with their start and end apart: 11, of which 4 were waited for; matrix products, arithmetic and copies ran while one was open for 2% of the time, Pallas kernels for 49%

profile of v2, /device:TPU:0, one launch (start us, length us, event | category | flops | bytes accessed | tf_op | source)
XLA Modules:
  0.0 194.9 jit_solution(12471732539821592163)
XLA Ops:
  0.0 1.4 fusion.3
  1.4 0.7 pad_add_fusion.refs_2_.refs_5_.refs_6_.refs_10_
  2.0 9.6 %prepare.1 = (bf16[16,384,384]{2,1,0:T(8,128)(2,1)}, bf16[18,24,384]{2,1,0:T(8,128)(2,1)}, bf16[18,24,384]{2,1,0:T(8,128)(2,1)}, bf16[16,16,384]{2,1,0:T(8,128)(...) custom-call(f32[16,16,24,384]{3,2,1,0:T(8,128)} %refs_14_.1, f32[1,384]{1,0:T(1,128)} %get-tuple-element.46.refs_1_, ...), custom_call_target="tpu_custom_call" | custom-call | flops 47185920 | bytes 14155776 | tf_op jit(solution)/shard_map/prepare/pallas_call | solution.py:83
  12.8 0.7 collective-permute-done.refs_3_.refs_4_
  13.7 0.6 constant_dynamic-update-slice_fusion.3
  14.3 2.9 %collective-permute-start.1 = (bf16[18,24,384]{2,1,0:T(8,128)(2,1)}, bf16[18,24,384]{2,1,0:T(8,128)(2,1)S(1)}, u32[]{:S(2)}, u32[]{:S(2)}) collective-permute-start(bf16[18,24,384]{2,1,0:T(8,128)(2,1)} %constant_dynamic-update-slice_fusion.3), channel_id=1, source_target_pairs={{0,2},{4,6},{2,0},{6,4},{1,3},{5,7},{3,1},{7,5},{8,10},{12,14},{10... | collective-permute-start | bytes 995336 | tf_op jit(solution)/shard_map/ppermute | solution.py:557
  17.3 0.6 constant_dynamic-update-slice_fusion.2
  17.9 0.7 collective-permute-start.2
  18.6 0.7 add_convert_fusion.refs_4_.refs_5_.refs_9_
  19.3 6.2 %collective-permute-done.1.refs_1_.refs_2_ = bf16[18,24,384]{2,1,0:T(8,128)(2,1)S(1)} collective-permute-done((bf16[18,24,384]{2,1,0:T(8,128)(2,1)}, bf16[18,24,384]{2,1,0:T(8,128)(2,1)S(1)}, u32[]{:S(2)}, u32[]{:S(2)}) %collective-permute-start.1) | collective-permute-done | bytes 331808 | tf_op jit(solution)/shard_map/ppermute | solution.py:557
  25.8 0.7 constant_dynamic-update-slice_fusion
  26.4 1.7 collective-permute-start.7
  28.1 37.4 %conv_first.2 = (bf16[8,384,384]{2,1,0:T(8,128)(2,1)}, bf16[9,24,384]{2,1,0:T(8,128)(2,1)}, bf16[9,24,384]{2,1,0:T(8,128)(2,1)}, bf16[8,16,384]{2,1,0:T(8,128)(2...) custom-call(bf16[16,384,384]{2,1,0:T(8,128)(2,1)} %get-tuple-element.19.refs_0_.refs_1_, ...), custom_call_target="tpu_custom_call" | custom-call | flops 24461180928 | bytes 9437184 | tf_op jit(solution)/shard_map/conv_first/pallas_call | solution.py:513
  65.7 0.9 copy-done.9
  66.6 37.7 %conv_first.3 = (bf16[8,384,384]{2,1,0:T(8,128)(2,1)}, bf16[9,24,384]{2,1,0:T(8,128)(2,1)}, bf16[9,24,384]{2,1,0:T(8,128)(2,1)}, bf16[8,16,384]{2,1,0:T(8,128)(2...) custom-call(bf16[2,472,384]{2,1,0:T(8,128)(2,1)} %copy-done.9, ...), custom_call_target="tpu_custom_call" | custom-call | flops 24461180928 | bytes 9437184 | tf_op jit(solution)/shard_map/conv_first/pallas_call | solution.py:513
  104.8 1.1 collective-permute-done.8.refs_4_
  106.2 0.7 collective-permute-start.5
  106.9 8.3 %collective-permute-start.4 = (bf16[9,24,384]{2,1,0:T(8,128)(2,1)S(1)}, bf16[9,24,384]{2,1,0:T(8,128)(2,1)S(1)}, u32[]{:S(2)}, u32[]{:S(2)}) collective-permute-start(bf16[9,24,384]{2,1,0:T(8,128)(2,1)S(1)} %bitcast_dynamic-update-slice_fusion.3), channel_id=1, source_target_pairs={{0,2},{4,6},{2,0},{6,4},{1,3},{5,7},{3,1},{7,5},{8,10},{12,14},{10... | collective-permute-start | bytes 497672 | tf_op jit(solution)/shard_map/ppermute | solution.py:557
  116.5 0.7 collective-permute-start.10
  117.2 3.0 %collective-permute-done.4.refs_1_.refs_6_ = bf16[9,24,384]{2,1,0:T(8,128)(2,1)S(1)} collective-permute-done((bf16[9,24,384]{2,1,0:T(8,128)(2,1)S(1)}, bf16[9,24,384]{2,1,0:T(8,128)(2,1)S(1)}, u32[]{:S(2)}, u32[]{:S(2)}) %collective-permute-start.4) | collective-permute-done | bytes 165920 | tf_op jit(solution)/shard_map/ppermute | solution.py:557
  120.5 1.5 collective-permute-start.6
  122.0 21.1 %conv_final.2.refs_15_ = f32[16,16,24,384]{3,2,1,0:T(8,128)} custom-call(bf16[8,384,384]{2,1,0:T(8,128)(2,1)} %get-tuple-element.32.refs_0_.refs_5_, bf16[9,24,384]{2,1,0:T(8,128)(2,1)} %copy-done.5, bf16[9,24,384]{2,1,0:T(8,128)(2,1)} %copy-done.4, bf16[8,16,384]{2,1,0:T(8,128)(2,1)} %copy-done.1, f32[4]{0:T(128)} %add_convert_fusion.refs_4_.refs_5_.refs_9_, ...), custom_call_target="tpu_custom_call" | custom-call | flops 12230590464 | bytes 4718592 | tf_op jit(solution)/shard_map/conv_final/pallas_call | solution.py:513
  143.2 0.6 copy-done.12
  144.2 50.5 %conv_final.3 = f32[16,16,24,384]{3,2,1,0:T(8,128)} custom-call(bf16[2,472,384]{2,1,0:T(8,128)(2,1)} %copy-done.10, bf16[8,384,384]{2,1,0:T(8,128)(2,1)} %get-tuple-element.28.refs_1_, bf16[9,24,384]{2,1,0:T(8,128)(2,1)} %copy-done.12, bf16[9,24,384]{2,1,0:T(8,128)(2,1)} %copy-done.14, ...), custom_call_target="tpu_custom_call", output_to_operand_aliasing={{}: (15, {})} | custom-call | flops 36691771392 | bytes 14155776 | tf_op jit(solution)/shard_map/conv_final/pallas_call | solution.py:513
  (78 shorter events, 4.3 us)
Async XLA Ops:
  0.0 12.2 %copy-start.7 = (f32[2,384]{1,0:T(2,128)S(1)}, f32[2,384]{1,0:T(2,128)}, u32[]{:S(2)}) copy-start(f32[2,384]{1,0:T(2,128)} %param.7) | copy-start | bytes 9220
  11.7 1.8 collective-permute-start
  13.5 14.6 %copy-start = (bf16[16,16,384]{2,1,0:T(8,128)(2,1)}, bf16[16,16,384]{2,1,0:T(8,128)(2,1)S(1)}, u32[]{:S(2)}) copy-start(bf16[16,16,384]{2,1,0:T(8,128)(2,1)S(1)} %collective-permute-done.refs_3_.refs_4_) | copy-start | bytes 589828
  14.3 11.2 %collective-permute-start.1 = (bf16[18,24,384]{2,1,0:T(8,128)(2,1)}, bf16[18,24,384]{2,1,0:T(8,128)(2,1)S(1)}, u32[]{:S(2)}, u32[]{:S(2)}) collective-permute-start(bf16[18,24,384]{2,1,0:T(8,128)(2,1)} %constant_dynamic-update-slice_fusion.3), channel_id=1, source_target_pairs={{0,2},{4,6},{2,0},{6,4},{1,3},{5,7},{3,1},{7,5},{8,10},{12,14},{10... | collective-permute-start | bytes 995336 | tf_op jit(solution)/shard_map/ppermute | solution.py:557
  17.9 7.6 %collective-permute-start.2 = (bf16[18,24,384]{2,1,0:T(8,128)(2,1)}, bf16[18,24,384]{2,1,0:T(8,128)(2,1)S(1)}, u32[]{:S(2)}, u32[]{:S(2)}) collective-permute-start(bf16[18,24,384]{2,1,0:T(8,128)(2,1)} %constant_dynamic-update-slice_fusion.2), channel_id=1, source_target_pairs={{2,4},{4,2},{3,5},{5,3},{10,12},{12,10},{11,13},{13,11},{18,20},{2... | collective-permute-start | bytes 995336 | tf_op jit(solution)/shard_map/ppermute | solution.py:557
  25.5 2.6 %copy-start.2 = (bf16[18,24,384]{2,1,0:T(8,128)(2,1)}, bf16[18,24,384]{2,1,0:T(8,128)(2,1)S(1)}, u32[]{:S(2)}) copy-start(bf16[18,24,384]{2,1,0:T(8,128)(2,1)S(1)} %collective-permute-done.1.refs_1_.refs_2_) | copy-start | bytes 995332
  25.6 2.5 %copy-start.3 = (bf16[18,24,384]{2,1,0:T(8,128)(2,1)}, bf16[18,24,384]{2,1,0:T(8,128)(2,1)S(1)}, u32[]{:S(2)}) copy-start(bf16[18,24,384]{2,1,0:T(8,128)(2,1)S(1)} %collective-permute-done.2.refs_2_.refs_3_) | copy-start | bytes 995332
  26.4 39.2 %collective-permute-start.7 = (bf16[2,472,384]{2,1,0:T(8,128)(2,1)}, bf16[2,472,384]{2,1,0:T(8,128)(2,1)S(1)}, u32[]{:S(2)}, u32[]{:S(2)}) collective-permute-start(bf16[2,472,384]{2,1,0:T(8,128)(2,1)} %constant_dynamic-update-slice_fusion), channel_id=1, source_target_pairs={{0,8},{8,16},{16,24},{24,0},{1,9},{9,17},{17,25},{25,1},{2,10},{10... | collective-permute-start | bytes 2174984 | tf_op jit(solution)/shard_map/ppermute | solution.py:591
  65.6 40.6 %copy-start.13 = (bf16[9,24,384]{2,1,0:T(8,128)(2,1)S(1)}, bf16[9,24,384]{2,1,0:T(8,128)(2,1)}, u32[]{:S(2)}) copy-start(bf16[9,24,384]{2,1,0:T(8,128)(2,1)} %get-tuple-element.26) | copy-start | bytes 497668
  65.6 41.3 %copy-start.11 = (bf16[9,24,384]{2,1,0:T(8,128)(2,1)S(1)}, bf16[9,24,384]{2,1,0:T(8,128)(2,1)}, u32[]{:S(2)}) copy-start(bf16[9,24,384]{2,1,0:T(8,128)(2,1)} %get-tuple-element.24) | copy-start | bytes 497668
  65.6 54.9 %copy-start.8 = (bf16[2,472,384]{2,1,0:T(8,128)(2,1)S(1)}, bf16[2,472,384]{2,1,0:T(8,128)(2,1)}, u32[]{:S(2)}) copy-start(bf16[2,472,384]{2,1,0:T(8,128)(2,1)} %get-tuple-element.23) | copy-start | bytes 2174980
  65.6 39.2 %collective-permute-start.3 = (bf16[8,16,384]{2,1,0:T(8,128)(2,1)}, bf16[8,16,384]{2,1,0:T(8,128)(2,1)S(1)}, u32[]{:S(2)}, u32[]{:S(2)}) collective-permute-start(bf16[8,16,384]{2,1,0:T(8,128)(2,1)} %get-tuple-element.25), channel_id=1, source_target_pairs={{0,1},{1,0},{2,3},{3,2},{4,5},{5,4},{6,7},{7,6},{8,9},{9,8},{10,11... | collective-permute-start | bytes 294920 | tf_op jit(solution)/shard_map/ppermute | solution.py:565
  65.7 0.9 copy-start.9
  104.3 1.7 collective-permute-start.8
  104.8 17.2 %copy-start.1 = (bf16[8,16,384]{2,1,0:T(8,128)(2,1)}, bf16[8,16,384]{2,1,0:T(8,128)(2,1)S(1)}, u32[]{:S(2)}) copy-start(bf16[8,16,384]{2,1,0:T(8,128)(2,1)S(1)} %collective-permute-done.3.refs_3_.refs_8_) | copy-start | bytes 294916
  106.0 37.2 %copy-start.6 = (bf16[8,16,384]{2,1,0:T(8,128)(2,1)}, bf16[8,16,384]{2,1,0:T(8,128)(2,1)S(1)}, u32[]{:S(2)}) copy-start(bf16[8,16,384]{2,1,0:T(8,128)(2,1)S(1)} %collective-permute-done.8.refs_4_) | copy-start | bytes 294916
  106.2 11.0 %collective-permute-start.5 = (bf16[9,24,384]{2,1,0:T(8,128)(2,1)S(1)}, bf16[9,24,384]{2,1,0:T(8,128)(2,1)S(1)}, u32[]{:S(2)}, u32[]{:S(2)}) collective-permute-start(bf16[9,24,384]{2,1,0:T(8,128)(2,1)S(1)} %bitcast_dynamic-update-slice_fusion.2), channel_id=1, source_target_pairs={{2,4},{4,2},{3,5},{5,3},{10,12},{12,10},{11,13},{13,11},{18,20},{2... | collective-permute-start | bytes 497672 | tf_op jit(solution)/shard_map/ppermute | solution.py:557
  106.9 13.4 %collective-permute-start.4 = (bf16[9,24,384]{2,1,0:T(8,128)(2,1)S(1)}, bf16[9,24,384]{2,1,0:T(8,128)(2,1)S(1)}, u32[]{:S(2)}, u32[]{:S(2)}) collective-permute-start(bf16[9,24,384]{2,1,0:T(8,128)(2,1)S(1)} %bitcast_dynamic-update-slice_fusion.3), channel_id=1, source_target_pairs={{0,2},{4,6},{2,0},{6,4},{1,3},{5,7},{3,1},{7,5},{8,10},{12,14},{10... | collective-permute-start | bytes 497672 | tf_op jit(solution)/shard_map/ppermute | solution.py:557
  115.8 27.3 %collective-permute-start.9 = (bf16[9,24,384]{2,1,0:T(8,128)(2,1)}, bf16[9,24,384]{2,1,0:T(8,128)(2,1)S(1)}, u32[]{:S(2)}, u32[]{:S(2)}) collective-permute-start(bf16[9,24,384]{2,1,0:T(8,128)(2,1)} %bitcast_dynamic-update-slice_fusion.1), channel_id=1, source_target_pairs={{0,2},{4,6},{2,0},{6,4},{1,3},{5,7},{3,1},{7,5},{8,10},{12,14},{10... | collective-permute-start | bytes 497672 | tf_op jit(solution)/shard_map/ppermute | solution.py:557
  116.5 26.7 %collective-permute-start.10 = (bf16[9,24,384]{2,1,0:T(8,128)(2,1)}, bf16[9,24,384]{2,1,0:T(8,128)(2,1)S(1)}, u32[]{:S(2)}, u32[]{:S(2)}) collective-permute-start(bf16[9,24,384]{2,1,0:T(8,128)(2,1)} %bitcast_dynamic-update-slice_fusion), channel_id=1, source_target_pairs={{2,4},{4,2},{3,5},{5,3},{10,12},{12,10},{11,13},{13,11},{18,20},{2... | collective-permute-start | bytes 497672 | tf_op jit(solution)/shard_map/ppermute | solution.py:557
  117.2 4.8 %copy-start.4 = (bf16[9,24,384]{2,1,0:T(8,128)(2,1)}, bf16[9,24,384]{2,1,0:T(8,128)(2,1)S(1)}, u32[]{:S(2)}) copy-start(bf16[9,24,384]{2,1,0:T(8,128)(2,1)S(1)} %collective-permute-done.5.refs_2_.refs_7_) | copy-start | bytes 497668
  120.3 1.7 copy-start.5
  120.5 22.7 %collective-permute-start.6 = (bf16[2,472,384]{2,1,0:T(8,128)(2,1)S(1)}, bf16[2,472,384]{2,1,0:T(8,128)(2,1)S(1)}, u32[]{:S(2)}, u32[]{:S(2)}) collective-permute-start(bf16[2,472,384]{2,1,0:T(8,128)(2,1)S(1)} %constant_dynamic-update-slice_fusion.1), channel_id=1, source_target_pairs={{0,8},{8,16},{16,24},{24,0},{1,9},{9,17},{17,25},{25,1},{2,10},{10... | collective-permute-start | bytes 2174984 | tf_op jit(solution)/shard_map/ppermute | solution.py:591
  143.2 1.0 copy-start.10
  (2 other events, 1.4 us)
